TPU v7x, 8 devices: a whole 2x2x1 slice. The times are simulated.
8 devices in a mesh: dp: 2 (over z, y), tp: 4 (over x, core).
Axes of the slice: x: 2, y: 2, z: 1, core: 2. Of those that a mesh axis runs over, the one named last changes fastest.
Arguments:
- x_in: bfloat16 [16, 2048, 1024], P('dp', 'tp'), parts along dimension 0
- ln_gain: float32 [2, 1024], replicated
- ln_bias: float32 [2, 1024], replicated
- w_qkv: bfloat16 [2, 1024, 3, 16, 64], P(None, None, None, 'tp')
- w_out: bfloat16 [2, 16, 64, 1024], P(None, 'tp')
- b_out: float32 [2, 1024], replicated
- w_up: bfloat16 [2, 1024, 4096], P(None, None, 'tp')
- b_up: float32 [2, 4096], P(None, 'tp')
- w_down: bfloat16 [2, 4096, 1024], P(None, 'tp')
- b_down: float32 [2, 1024], replicated
Outputs:
- output: bfloat16 [16, 2048, 1024], P('dp', 'tp'), parts along dimension 0
There are 2 independent parts. A program takes and returns all parts, laid end to end along the dimension named above; an argument that names none is the same for every part.
All inputs are finite; a program needn't handle non-finite values.
Results may differ from a plain program's by a relative error of at most 0.0128649.
Values are sent between devices in bfloat16 or wider.
A program may use at most 1 GiB of HBM per device.

v0:
```python
import jax
import jax.numpy as jnp
from jax import lax
from jax.sharding import PartitionSpec as P

LN_EPS = 1e-5


def layer_norm(residual, gain, bias):
    row_mean = jnp.mean(residual, axis=-1, keepdims=True)
    centered = residual - row_mean
    row_var = jnp.mean(centered * centered, axis=-1, keepdims=True)
    return (centered * lax.rsqrt(row_var + LN_EPS) * gain + bias).astype(jnp.bfloat16)


def query_block(batch, heads, q_len, k_len):
    block = q_len
    while block % 2 == 0 and block > 16 and batch * heads * block * k_len > 2 ** 24:
        block = block // 2
    return block


def causal_attention(queries, keys, values, q_start):
    batch, q_len, heads, head_dim = queries.shape
    k_len = keys.shape[1]
    block = query_block(batch, heads, q_len, k_len)
    inv_sqrt = head_dim ** -0.5
    key_pos = jnp.arange(k_len)

    def one_block(index):
        q_blk = lax.dynamic_slice_in_dim(queries, index * block, block, axis=1)
        scores = jnp.einsum('bqhe,bkhe->bhqk', q_blk, keys, preferred_element_type=jnp.float32) * inv_sqrt
        q_pos = q_start + index * block + jnp.arange(block)
        scores = jnp.where(key_pos[None, :] <= q_pos[:, None], scores, -jnp.inf)
        attn_prob = jax.nn.softmax(scores, axis=-1).astype(jnp.bfloat16)
        return jnp.einsum('bhqk,bkhe->bqhe', attn_prob, values, preferred_element_type=jnp.float32).astype(jnp.bfloat16)

    out_blocks = lax.map(one_block, jnp.arange(q_len // block))
    return jnp.moveaxis(out_blocks, 0, 1).reshape(batch, q_len, heads, head_dim)


def solution(mesh):
    tp_size = mesh.shape['tp']
    act_spec = P('dp', 'tp', None)

    def layer(residual, ln_gain, ln_bias, w_qkv, w_out, w_up, bias_up, w_down, bias_sum):
        normed = layer_norm(residual, ln_gain, ln_bias)
        gathered = lax.all_gather(normed, 'tp', axis=1, tiled=True)
        qkv_all = jnp.einsum('bsd,dthe->bsthe', gathered, w_qkv, preferred_element_type=jnp.float32).astype(jnp.bfloat16)
        attn_out = causal_attention(qkv_all[:, :, 0], qkv_all[:, :, 1], qkv_all[:, :, 2], 0)
        partial = jnp.einsum('bshe,hed->bsd', attn_out, w_out, preferred_element_type=jnp.float32)
        hidden = jnp.einsum('bsd,df->bsf', gathered, w_up, preferred_element_type=jnp.float32) + bias_up
        gelu_out = jax.nn.gelu(hidden, approximate=True).astype(jnp.bfloat16)
        partial = partial + jnp.einsum('bsf,fd->bsd', gelu_out, w_down, preferred_element_type=jnp.float32)
        received = lax.all_to_all(partial.astype(jnp.bfloat16), 'tp', 1, 1, tiled=True)
        batch, seq_len, width = received.shape
        summed = jnp.sum(received.reshape(batch, tp_size, seq_len // tp_size, width), axis=1, dtype=jnp.float32)
        return residual + (summed + bias_sum)

    def local_fn(x_in, ln_gain, ln_bias, w_qkv, w_out, b_out, w_up, b_up, w_down, b_down):
        residual = x_in.astype(jnp.float32)
        for layer_idx in range(w_qkv.shape[0]):
            residual = layer(residual, ln_gain[layer_idx], ln_bias[layer_idx], w_qkv[layer_idx], w_out[layer_idx],
                             w_up[layer_idx], b_up[layer_idx], w_down[layer_idx], b_out[layer_idx] + b_down[layer_idx])
        return residual.astype(jnp.bfloat16)

    in_specs = (act_spec, P(), P(), P(None, None, None, 'tp', None), P(None, 'tp', None, None), P(),
                P(None, None, 'tp'), P(None, 'tp'), P(None, 'tp', None), P())
    return jax.shard_map(local_fn, mesh=mesh, in_specs=in_specs, out_specs=act_spec, check_vma=False)
```

profile of v0, /device:TPU:0, one launch (start us, length us, event | category | flops | bytes accessed | tf_op | source)
XLA Modules:
  0.0 2709.2 jit_solution(12716866784484289931)
XLA Ops:
  9.4 4.5 convert_reduce_fusion.2
  14.0 6.4 fusion.80
  20.4 5.2 fusion.83
  26.2 201.7 %all-gather.3.cloned.1.call-done = bf16[8,2048,1024]{2,1,0:T(8,128)(2,1)} async-done(((bf16[8,512,1024]{2,1,0:T(8,128)(2,1)}), bf16[8,2048,1024]{2,1,0:T(8,128)(2,1)}) %all-gather.3.cloned.1.call-update) | async-done | bytes 33554448 | tf_op jit(solution)/shard_map/all_gather | solution.py:48
  227.9 33.0 %fusion.86 = bf16[8,2048,3,4,64]{1,4,3,2,0:T(8,128)(2,1)} fusion(bf16[8,2048,1024]{2,1,0:T(8,128)(2,1)} %all-gather.3.cloned.1.call-done, bf16[2,1024,3,4,64]{1,4,3,2,0:T(8,128)(2,1)S(1)} %copy-done.11), kind=kOutput, calls=%fused_computation.91 | convolution fusion | flops 25782386688 | bytes 60293120 | tf_op jit(solution)/shard_map/bsd,dthe->bsthe/dot_general | solution.py:49
  260.9 17.0 slice_bitcast_fusion.3
  277.8 4.5 broadcast.77.clone
  282.3 470.9 %while.22 = (s32[]{:T(128)}, bf16[8,8,256,4,64]{2,4,3,1,0:T(8,128)(2,1)}, s32[8]{0:T(128)S(1)}, bf16[8,2048,4,64]{1,3,2,0:T(8,128)(2,1)}, bf16[8,2048,4,64]{1,3,...) while((s32[]{:T(128)}, ...), condition=%wide.region_5.6_spmd.clone, body=%wide.region_2.5_spmd.clone.sunk | while | flops 4396681216 | bytes 154208432 | solution.py:38
  284.4 30.4 %fusion.199 = (f32[8,4,256]{2,1,0:T(4,128)S(1)}, f32[8,4,256,2048]{3,2,1,0:T(8,128)}) fusion(pred[256,2048]{1,0:T(8,128)(4,1)S(1)} %iota_compare_fusion.4, bf16[8,2048,4,64]{1,3,2,0:T(8,128)(2,1)} %get-tuple-element.257, bf16[8,2048,4,64]{1,3,2,0:T(8,128)(2,1)} %get-tuple-element.256, s32[]{:T(128)S(6)} %select_n.42), kind=kOutput, calls=%fused_computation.132.clone.1 | convolution fusion | flops 2214594560 | bytes 77103104 | tf_op jit(solution)/shard_map/while/body/eval_jaxpr/sub | solution.py:35
  314.7 26.8 fusion.200
  343.2 30.4 %fusion.199 = (f32[8,4,256]{2,1,0:T(4,128)S(1)}, f32[8,4,256,2048]{3,2,1,0:T(8,128)}) fusion(pred[256,2048]{1,0:T(8,128)(4,1)S(1)} %iota_compare_fusion.4, bf16[8,2048,4,64]{1,3,2,0:T(8,128)(2,1)} %get-tuple-element.257, bf16[8,2048,4,64]{1,3,2,0:T(8,128)(2,1)} %get-tuple-element.256, s32[]{:T(128)S(6)} %select_n.42), kind=kOutput, calls=%fused_computation.132.clone.1 | convolution fusion | flops 2214594560 | bytes 77103104 | tf_op jit(solution)/shard_map/while/body/eval_jaxpr/sub | solution.py:35
  373.5 26.8 fusion.200
  402.0 30.4 %fusion.199 = (f32[8,4,256]{2,1,0:T(4,128)S(1)}, f32[8,4,256,2048]{3,2,1,0:T(8,128)}) fusion(pred[256,2048]{1,0:T(8,128)(4,1)S(1)} %iota_compare_fusion.4, bf16[8,2048,4,64]{1,3,2,0:T(8,128)(2,1)} %get-tuple-element.257, bf16[8,2048,4,64]{1,3,2,0:T(8,128)(2,1)} %get-tuple-element.256, s32[]{:T(128)S(6)} %select_n.42), kind=kOutput, calls=%fused_computation.132.clone.1 | convolution fusion | flops 2214594560 | bytes 77103104 | tf_op jit(solution)/shard_map/while/body/eval_jaxpr/sub | solution.py:35
  432.3 26.8 fusion.200
  460.8 30.4 %fusion.199 = (f32[8,4,256]{2,1,0:T(4,128)S(1)}, f32[8,4,256,2048]{3,2,1,0:T(8,128)}) fusion(pred[256,2048]{1,0:T(8,128)(4,1)S(1)} %iota_compare_fusion.4, bf16[8,2048,4,64]{1,3,2,0:T(8,128)(2,1)} %get-tuple-element.257, bf16[8,2048,4,64]{1,3,2,0:T(8,128)(2,1)} %get-tuple-element.256, s32[]{:T(128)S(6)} %select_n.42), kind=kOutput, calls=%fused_computation.132.clone.1 | convolution fusion | flops 2214594560 | bytes 77103104 | tf_op jit(solution)/shard_map/while/body/eval_jaxpr/sub | solution.py:35
  491.1 26.8 fusion.200
  519.6 30.4 %fusion.199 = (f32[8,4,256]{2,1,0:T(4,128)S(1)}, f32[8,4,256,2048]{3,2,1,0:T(8,128)}) fusion(pred[256,2048]{1,0:T(8,128)(4,1)S(1)} %iota_compare_fusion.4, bf16[8,2048,4,64]{1,3,2,0:T(8,128)(2,1)} %get-tuple-element.257, bf16[8,2048,4,64]{1,3,2,0:T(8,128)(2,1)} %get-tuple-element.256, s32[]{:T(128)S(6)} %select_n.42), kind=kOutput, calls=%fused_computation.132.clone.1 | convolution fusion | flops 2214594560 | bytes 77103104 | tf_op jit(solution)/shard_map/while/body/eval_jaxpr/sub | solution.py:35
  549.9 26.8 fusion.200
  578.4 30.4 %fusion.199 = (f32[8,4,256]{2,1,0:T(4,128)S(1)}, f32[8,4,256,2048]{3,2,1,0:T(8,128)}) fusion(pred[256,2048]{1,0:T(8,128)(4,1)S(1)} %iota_compare_fusion.4, bf16[8,2048,4,64]{1,3,2,0:T(8,128)(2,1)} %get-tuple-element.257, bf16[8,2048,4,64]{1,3,2,0:T(8,128)(2,1)} %get-tuple-element.256, s32[]{:T(128)S(6)} %select_n.42), kind=kOutput, calls=%fused_computation.132.clone.1 | convolution fusion | flops 2214594560 | bytes 77103104 | tf_op jit(solution)/shard_map/while/body/eval_jaxpr/sub | solution.py:35
  608.7 26.8 fusion.200
  637.2 30.4 %fusion.199 = (f32[8,4,256]{2,1,0:T(4,128)S(1)}, f32[8,4,256,2048]{3,2,1,0:T(8,128)}) fusion(pred[256,2048]{1,0:T(8,128)(4,1)S(1)} %iota_compare_fusion.4, bf16[8,2048,4,64]{1,3,2,0:T(8,128)(2,1)} %get-tuple-element.257, bf16[8,2048,4,64]{1,3,2,0:T(8,128)(2,1)} %get-tuple-element.256, s32[]{:T(128)S(6)} %select_n.42), kind=kOutput, calls=%fused_computation.132.clone.1 | convolution fusion | flops 2214594560 | bytes 77103104 | tf_op jit(solution)/shard_map/while/body/eval_jaxpr/sub | solution.py:35
  667.6 26.8 fusion.200
  696.0 30.4 %fusion.199 = (f32[8,4,256]{2,1,0:T(4,128)S(1)}, f32[8,4,256,2048]{3,2,1,0:T(8,128)}) fusion(pred[256,2048]{1,0:T(8,128)(4,1)S(1)} %iota_compare_fusion.4, bf16[8,2048,4,64]{1,3,2,0:T(8,128)(2,1)} %get-tuple-element.257, bf16[8,2048,4,64]{1,3,2,0:T(8,128)(2,1)} %get-tuple-element.256, s32[]{:T(128)S(6)} %select_n.42), kind=kOutput, calls=%fused_computation.132.clone.1 | convolution fusion | flops 2214594560 | bytes 77103104 | tf_op jit(solution)/shard_map/while/body/eval_jaxpr/sub | solution.py:35
  726.4 26.8 fusion.200
  753.2 7.8 copy.27
  761.0 60.0 %fusion.184 = bf16[8,2048,1024]{2,1,0:T(8,128)(2,1)} fusion(f32[1024]{0:T(1024)S(1)} %bitcast.181, bf16[8,2048,1024]{2,1,0:T(8,128)(2,1)} %all-gather.3.cloned.1.call-done, bf16[2,1024,1024]{2,1,0:T(8,128)(2,1)} %param.20), kind=kOutput, calls=%fused_computation.55.clone.clone.2 | convolution fusion | flops 34527510528 | bytes 69210112 | tf_op jit(solution)/shard_map/bsd,df->bsf/dot_general | solution.py:52
  821.0 46.1 %fusion.76 = f32[8,2048,1024]{2,1,0:T(8,128)} fusion(bf16[2,1024,1024]{2,1,0:T(8,128)(2,1)} %param.22, bf16[8,2048,1024]{2,1,0:T(8,128)(2,1)} %fusion.184), kind=kOutput, calls=%fused_computation.75 | convolution fusion | flops 34359738368 | bytes 102760448 | tf_op jit(solution)/shard_map/bsf,fd->bsd/dot_general | solution.py:54
  867.1 40.5 %fusion.69 = bf16[8,2048,1024]{2,1,0:T(8,128)(2,1)} fusion(f32[8,2048,1024]{2,1,0:T(8,128)} %fusion.76, bf16[8,2048,4,64]{1,3,2,0:T(8,128)(2,1)} %bitcast.170, bf16[2,4,64,1024]{3,2,1,0:T(8,128)(2,1)S(1)} %copy-done.12), kind=kOutput, calls=%fused_computation.69 | convolution fusion | flops 8623489024 | bytes 109576192 | tf_op jit(solution)/shard_map/bshe,hed->bsd/dot_general | solution.py:51
  907.6 30.9 %copy.18 = bf16[8,2048,1024]{2,0,1:T(8,128)(2,1)} copy(bf16[8,2048,1024]{2,1,0:T(8,128)(2,1)} %fusion.69) | data formatting | bytes 67108864 | tf_op jit(solution)/shard_map/convert_element_type | solution.py:55
  938.6 9.9 all-to-all-start
  949.1 361.8 %all-to-all-done = bf16[8,2048,1024]{2,0,1:T(8,128)(2,1)} async-done(((bf16[8,2048,1024]{2,0,1:T(8,128)(2,1)}), bf16[8,2048,1024]{2,0,1:T(8,128)(2,1)}, u32[]{:S(2)}, u32[]{:S(2)}) %all-to-all-start) | async-done | bytes 33554464 | tf_op jit(solution)/shard_map/all_to_all | solution.py:55
  1310.9 19.0 convert_reduce_fusion.1
  1330.0 15.0 fusion.124
  1345.0 9.8 multiply_reduce_fusion
  1354.9 11.8 add_convert_fusion
  1366.7 199.5 %all-gather.5.cloned.1.call-done = bf16[8,2048,1024]{2,1,0:T(8,128)(2,1)} async-done(((bf16[8,512,1024]{2,1,0:T(8,128)(2,1)}), bf16[8,2048,1024]{2,1,0:T(8,128)(2,1)}) %all-gather.5.cloned.1.call-update) | async-done | bytes 33554448 | tf_op jit(solution)/shard_map/all_gather | solution.py:48
  1566.2 33.6 %fusion.89 = bf16[8,2048,3,4,64]{1,4,3,2,0:T(8,128)(2,1)} fusion(bf16[8,2048,1024]{2,1,0:T(8,128)(2,1)} %all-gather.5.cloned.1.call-done, bf16[2,1024,3,4,64]{1,4,3,2,0:T(8,128)(2,1)} %param.17), kind=kOutput, calls=%fused_computation.92 | convolution fusion | flops 25782386688 | bytes 60293120 | tf_op jit(solution)/shard_map/bsd,dthe->bsthe/dot_general | solution.py:49
  1599.8 17.0 slice_bitcast_fusion
  1616.7 4.5 broadcast.77
  1621.2 469.9 %while.23 = (s32[]{:T(128)}, bf16[8,8,256,4,64]{2,4,3,1,0:T(8,128)(2,1)}, s32[8]{0:T(128)S(1)}, bf16[8,2048,4,64]{1,3,2,0:T(8,128)(2,1)}, bf16[8,2048,4,64]{1,3,...) while((s32[]{:T(128)}, ...), condition=%wide.region_12.13_spmd.clone, body=%wide.region_9.12_spmd.clone.sunk | while | flops 4396681216 | bytes 154208432 | solution.py:38
  1623.1 30.4 %fusion.204 = (f32[8,4,256]{2,1,0:T(4,128)S(1)}, f32[8,4,256,2048]{3,2,1,0:T(8,128)}) fusion(pred[256,2048]{1,0:T(8,128)(4,1)S(1)} %iota_compare_fusion.5, bf16[8,2048,4,64]{1,3,2,0:T(8,128)(2,1)} %get-tuple-element.287, bf16[8,2048,4,64]{1,3,2,0:T(8,128)(2,1)} %get-tuple-element.286, s32[]{:T(128)S(6)} %select_n.44), kind=kOutput, calls=%fused_computation.133.clone.1 | convolution fusion | flops 2214594560 | bytes 77103104 | tf_op jit(solution)/shard_map/while/body/eval_jaxpr/sub | solution.py:35
  1653.4 26.8 fusion.205
  1681.7 30.4 %fusion.204 = (f32[8,4,256]{2,1,0:T(4,128)S(1)}, f32[8,4,256,2048]{3,2,1,0:T(8,128)}) fusion(pred[256,2048]{1,0:T(8,128)(4,1)S(1)} %iota_compare_fusion.5, bf16[8,2048,4,64]{1,3,2,0:T(8,128)(2,1)} %get-tuple-element.287, bf16[8,2048,4,64]{1,3,2,0:T(8,128)(2,1)} %get-tuple-element.286, s32[]{:T(128)S(6)} %select_n.44), kind=kOutput, calls=%fused_computation.133.clone.1 | convolution fusion | flops 2214594560 | bytes 77103104 | tf_op jit(solution)/shard_map/while/body/eval_jaxpr/sub | solution.py:35
  1712.1 26.8 fusion.205
  1740.4 30.4 %fusion.204 = (f32[8,4,256]{2,1,0:T(4,128)S(1)}, f32[8,4,256,2048]{3,2,1,0:T(8,128)}) fusion(pred[256,2048]{1,0:T(8,128)(4,1)S(1)} %iota_compare_fusion.5, bf16[8,2048,4,64]{1,3,2,0:T(8,128)(2,1)} %get-tuple-element.287, bf16[8,2048,4,64]{1,3,2,0:T(8,128)(2,1)} %get-tuple-element.286, s32[]{:T(128)S(6)} %select_n.44), kind=kOutput, calls=%fused_computation.133.clone.1 | convolution fusion | flops 2214594560 | bytes 77103104 | tf_op jit(solution)/shard_map/while/body/eval_jaxpr/sub | solution.py:35
  1770.8 26.8 fusion.205
  1799.1 30.4 %fusion.204 = (f32[8,4,256]{2,1,0:T(4,128)S(1)}, f32[8,4,256,2048]{3,2,1,0:T(8,128)}) fusion(pred[256,2048]{1,0:T(8,128)(4,1)S(1)} %iota_compare_fusion.5, bf16[8,2048,4,64]{1,3,2,0:T(8,128)(2,1)} %get-tuple-element.287, bf16[8,2048,4,64]{1,3,2,0:T(8,128)(2,1)} %get-tuple-element.286, s32[]{:T(128)S(6)} %select_n.44), kind=kOutput, calls=%fused_computation.133.clone.1 | convolution fusion | flops 2214594560 | bytes 77103104 | tf_op jit(solution)/shard_map/while/body/eval_jaxpr/sub | solution.py:35
  1829.5 26.8 fusion.205
  1857.8 30.4 %fusion.204 = (f32[8,4,256]{2,1,0:T(4,128)S(1)}, f32[8,4,256,2048]{3,2,1,0:T(8,128)}) fusion(pred[256,2048]{1,0:T(8,128)(4,1)S(1)} %iota_compare_fusion.5, bf16[8,2048,4,64]{1,3,2,0:T(8,128)(2,1)} %get-tuple-element.287, bf16[8,2048,4,64]{1,3,2,0:T(8,128)(2,1)} %get-tuple-element.286, s32[]{:T(128)S(6)} %select_n.44), kind=kOutput, calls=%fused_computation.133.clone.1 | convolution fusion | flops 2214594560 | bytes 77103104 | tf_op jit(solution)/shard_map/while/body/eval_jaxpr/sub | solution.py:35
  1888.2 26.8 fusion.205
  1916.5 30.4 %fusion.204 = (f32[8,4,256]{2,1,0:T(4,128)S(1)}, f32[8,4,256,2048]{3,2,1,0:T(8,128)}) fusion(pred[256,2048]{1,0:T(8,128)(4,1)S(1)} %iota_compare_fusion.5, bf16[8,2048,4,64]{1,3,2,0:T(8,128)(2,1)} %get-tuple-element.287, bf16[8,2048,4,64]{1,3,2,0:T(8,128)(2,1)} %get-tuple-element.286, s32[]{:T(128)S(6)} %select_n.44), kind=kOutput, calls=%fused_computation.133.clone.1 | convolution fusion | flops 2214594560 | bytes 77103104 | tf_op jit(solution)/shard_map/while/body/eval_jaxpr/sub | solution.py:35
  1946.9 26.8 fusion.205
  1975.2 30.4 %fusion.204 = (f32[8,4,256]{2,1,0:T(4,128)S(1)}, f32[8,4,256,2048]{3,2,1,0:T(8,128)}) fusion(pred[256,2048]{1,0:T(8,128)(4,1)S(1)} %iota_compare_fusion.5, bf16[8,2048,4,64]{1,3,2,0:T(8,128)(2,1)} %get-tuple-element.287, bf16[8,2048,4,64]{1,3,2,0:T(8,128)(2,1)} %get-tuple-element.286, s32[]{:T(128)S(6)} %select_n.44), kind=kOutput, calls=%fused_computation.133.clone.1 | convolution fusion | flops 2214594560 | bytes 77103104 | tf_op jit(solution)/shard_map/while/body/eval_jaxpr/sub | solution.py:35
  2005.6 26.8 fusion.205
  2033.9 30.4 %fusion.204 = (f32[8,4,256]{2,1,0:T(4,128)S(1)}, f32[8,4,256,2048]{3,2,1,0:T(8,128)}) fusion(pred[256,2048]{1,0:T(8,128)(4,1)S(1)} %iota_compare_fusion.5, bf16[8,2048,4,64]{1,3,2,0:T(8,128)(2,1)} %get-tuple-element.287, bf16[8,2048,4,64]{1,3,2,0:T(8,128)(2,1)} %get-tuple-element.286, s32[]{:T(128)S(6)} %select_n.44), kind=kOutput, calls=%fused_computation.133.clone.1 | convolution fusion | flops 2214594560 | bytes 77103104 | tf_op jit(solution)/shard_map/while/body/eval_jaxpr/sub | solution.py:35
  2064.3 26.8 fusion.205
  2091.1 7.8 copy.28
  2098.9 59.8 %fusion.180 = bf16[8,2048,1024]{2,1,0:T(8,128)(2,1)} fusion(f32[1024]{0:T(1024)S(1)} %bitcast.180, bf16[8,2048,1024]{2,1,0:T(8,128)(2,1)} %all-gather.5.cloned.1.call-done, bf16[2,1024,1024]{2,1,0:T(8,128)(2,1)} %param.20), kind=kOutput, calls=%fused_computation.63.clone.clone.2 | convolution fusion | flops 34527510528 | bytes 69210112 | tf_op jit(solution)/shard_map/bsd,df->bsf/dot_general | solution.py:52
  2158.7 46.1 %fusion.74 = f32[8,2048,1024]{2,1,0:T(8,128)} fusion(bf16[2,1024,1024]{2,1,0:T(8,128)(2,1)} %param.22, bf16[8,2048,1024]{2,1,0:T(8,128)(2,1)} %fusion.180), kind=kOutput, calls=%fused_computation.74 | convolution fusion | flops 34359738368 | bytes 102760448 | tf_op jit(solution)/shard_map/bsf,fd->bsd/dot_general | solution.py:54
  2204.8 40.5 %fusion.68 = bf16[8,2048,1024]{2,1,0:T(8,128)(2,1)} fusion(f32[8,2048,1024]{2,1,0:T(8,128)} %fusion.74, bf16[8,2048,4,64]{1,3,2,0:T(8,128)(2,1)} %bitcast.169, bf16[2,4,64,1024]{3,2,1,0:T(8,128)(2,1)S(1)} %copy-done.13), kind=kOutput, calls=%fused_computation.67 | convolution fusion | flops 8623489024 | bytes 109576192 | tf_op jit(solution)/shard_map/bshe,hed->bsd/dot_general | solution.py:51
  2245.3 31.0 %copy.21 = bf16[8,2048,1024]{2,0,1:T(8,128)(2,1)} copy(bf16[8,2048,1024]{2,1,0:T(8,128)(2,1)} %fusion.68) | data formatting | bytes 67108864 | tf_op jit(solution)/shard_map/convert_element_type | solution.py:55
  2276.4 381.8 %all_to_all.10 = bf16[8,2048,1024]{2,0,1:T(8,128)(2,1)} all-to-all(bf16[8,2048,1024]{2,0,1:T(8,128)(2,1)} %copy.21), channel_id=1, replica_groups=mesh['dp'=2,'tp'=4] {'tp'}, dimensions={1} | all-to-all | bytes 67108864 | tf_op jit(solution)/shard_map/all_to_all | solution.py:55
  2658.2 24.9 convert_reduce_fusion
  2683.2 18.8 fusion.85
  (109 shorter events, 19.3 us)
Async XLA Ops:
  6.5 221.4 %all-gather.3.cloned.1.call-start = ((), (), s32[]{:S(2)}) async-start(), calls=%async_computation.2 | async-start | bytes 41943040 | tf_op jit(solution)/shard_map/all_gather | solution.py:48
  6.5 13.8 slice-start.4
  13.9 6.5 slice-start.5
  14.0 11.6 copy-start.8
  14.0 214.0 %copy-start.11 = (bf16[2,1024,3,4,64]{1,4,3,2,0:T(8,128)(2,1)S(1)}, bf16[2,1024,3,4,64]{1,4,3,2,0:T(8,128)(2,1)}, u32[]{:S(2)}) copy-start(bf16[2,1024,3,4,64]{1,4,3,2,0:T(8,128)(2,1)} %param.17) | copy-start | bytes 9437188
  753.2 7.8 copy-start.10
  821.0 46.1 %copy-start.12 = (bf16[2,4,64,1024]{3,2,1,0:T(8,128)(2,1)S(1)}, bf16[2,4,64,1024]{3,2,1,0:T(8,128)(2,1)}, u32[]{:S(2)}) copy-start(bf16[2,4,64,1024]{3,2,1,0:T(8,128)(2,1)} %param.18) | copy-start | bytes 3145732
  938.5 9.9 copy-start.6
  938.5 9.9 copy-start.7
  938.6 372.3 %all-to-all-start = ((bf16[8,2048,1024]{2,0,1:T(8,128)(2,1)}), bf16[8,2048,1024]{2,0,1:T(8,128)(2,1)}, u32[]{:S(2)}, u32[]{:S(2)}) async-start(bf16[8,2048,1024]{2,0,1:T(8,128)(2,1)} %copy.18), calls=%async_computation | async-start | bytes 67108864 | tf_op jit(solution)/shard_map/all_to_all | solution.py:55
  948.4 617.8 %all-gather.5.cloned.1.call-start = ((), (), s32[]{:S(2)}) async-start(), calls=%async_computation.3 | async-start | bytes 41943040 | tf_op jit(solution)/shard_map/all_gather | solution.py:48
  949.1 405.7 %copy-start.1 = (f32[1,1024]{1,0:T(1,128)}, f32[1,1024]{1,0:T(1,128)S(1)}, u32[]{:S(2)}) copy-start(f32[1,1024]{1,0:T(1,128)S(1)} %get-tuple-element.144) | copy-start | bytes 12292
  1329.9 24.9 copy-start
  1329.9 15.0 slice-start.6
  1330.0 15.0 slice-start.7
  1345.0 9.9 copy-start.3
  1345.0 9.9 copy-start.4
  2091.1 7.8 copy-start.9
  2158.7 46.1 %copy-start.13 = (bf16[2,4,64,1024]{3,2,1,0:T(8,128)(2,1)S(1)}, bf16[2,4,64,1024]{3,2,1,0:T(8,128)(2,1)}, u32[]{:S(2)}) copy-start(bf16[2,4,64,1024]{3,2,1,0:T(8,128)(2,1)} %param.18) | copy-start | bytes 3145732
  2276.3 406.8 %slice-start = ((s8[16777216]{0:T(1024)(128)(4,1)}), s8[4194304]{0:T(1024)(128)(4,1)S(1)}, s32[]{:S(2)}) async-start(s8[16777216]{0:T(1024)(128)(4,1)} %bitcast.160), calls=%async_computation.4 | async-start | bytes 8388608
  2276.4 406.8 %slice-start.1 = ((s8[16777216]{0:T(1024)(128)(4,1)}), s8[4194304]{0:T(1024)(128)(4,1)S(1)}, s32[]{:S(2)}) async-start(s8[16777216]{0:T(1024)(128)(4,1)} %bitcast.160), calls=%async_computation.5 | async-start | bytes 8388608
  2276.4 406.8 %slice-start.2 = ((s8[16777216]{0:T(1024)(128)(4,1)}), s8[4194304]{0:T(1024)(128)(4,1)S(1)}, s32[]{:S(2)}) async-start(s8[16777216]{0:T(1024)(128)(4,1)} %bitcast.160), calls=%async_computation.6 | async-start | bytes 8388608
  2658.2 25.0 slice-start.3
  2658.2 25.0 copy-start.2
  2658.2 25.0 copy-start.5
Sparse Core Ops, SparseCore 0:
  25.7 202.1 all-gather.2
  1366.8 199.3 all-gather.4
where the time goes:
time: 2720 us; the launch traced here: 2710 us
  matrix products  1270 us (47%)
  waiting for transfers between devices  763 us (28%)
  blocking collectives  382 us (14%)
  local copies, waits for them, and re-layouts  133 us (5%)
  other arithmetic  122 us (4%)
    sub x16, matrix products, one_block(): attn_prob = jax.nn.softmax(scores, axis=-1).astype(jnp.bfloat16)  486 us
    dot_general x16, matrix products, one_block(): jnp.einsum('bhqk,bkhe->bqhe', attn_prob, values, preferred_element_type=j...  429 us
    all_gather x2, waiting for transfers between devices, layer(): gathered = lax.all_gather(normed, 'tp', axis=1, tiled=True)  401 us
    all_to_all x1, blocking collectives, layer(): lax.all_to_all(partial.astype(jnp.bfloat16), 'tp', 1, 1, tiled=True)  382 us
    all_to_all x1, waiting for transfers between devices, layer(): lax.all_to_all(partial.astype(jnp.bfloat16), 'tp', 1, 1, tiled=True)  362 us
    dot_general x2, matrix products, layer(): jnp.einsum('bsd,df->bsf', gathered, w_up, preferred_element_type=jnp.floa...  120 us
    dot_general x2, matrix products, layer(): jnp.einsum('bsf,fd->bsd', gelu_out, w_down, preferred_element_type=jnp.fl...  92.1 us
    dot_general x2, matrix products, layer(): jnp.einsum('bshe,hed->bsd', attn_out, w_out, preferred_element_type=jnp.f...  81.1 us
  transfers between devices with their start and end apart: 3, of which 3 were waited for; matrix products, arithmetic and copies ran while one was open for 0% of the time, Pallas kernels for 0%

commit v1 on v0

v1 whole, which is shorter than its diff:
```python
import functools
import math

import jax
import jax.numpy as jnp
from jax import lax
from jax.experimental import pallas as pl
from jax.experimental.pallas import tpu as pltpu
from jax.sharding import PartitionSpec as P


LN_EPS = 1e-5
BLOCK_TOKENS = 512
TP_SIZE = 4
BLOCK_Q = 256
BLOCK_K = 256
VMEM_LIMIT = 58 * 1024 * 1024
SQRT_2_OVER_PI = math.sqrt(2.0 / math.pi)
LOG2_E = math.log2(math.e)


def layer_norm(residual, gain, bias):
    row_mean = jnp.mean(residual, axis=-1, keepdims=True)
    centered = residual - row_mean
    row_var = jnp.mean(centered * centered, axis=-1, keepdims=True)
    return (centered * lax.rsqrt(row_var + LN_EPS) * gain + bias).astype(jnp.bfloat16)


def gelu_tanh(x):
    inner = x * (SQRT_2_OVER_PI + (SQRT_2_OVER_PI * 0.044715) * (x * x))
    half = 0.5 * x
    return half + half * jnp.tanh(inner)


def dot(a, b):
    return lax.dot_general(a, b, (((1,), (0,)), ((), ())), preferred_element_type=jnp.float32)


def cost(flops, nbytes):
    return pl.CostEstimate(flops=flops, transcendentals=0, bytes_accessed=nbytes)


def start_qkv_copies(w_hbm, w_vmem, sem):
    parts, rows, _ = w_hbm.shape
    chunks = w_vmem.shape[0]
    for i in range(parts):
        half, chunk = divmod(i, chunks)
        pltpu.make_async_copy(w_hbm.at[i], w_vmem.at[chunk, pl.ds(half * rows, rows)], sem).start()


def wait_qkv_copies(w_hbm, w_vmem, sem):
    parts, rows, _ = w_hbm.shape
    chunks = w_vmem.shape[0]
    for i in range(parts):
        half, chunk = divmod(i, chunks)
        pltpu.make_async_copy(w_hbm.at[i], w_vmem.at[chunk, pl.ds(half * rows, rows)], sem).wait()


def project_qkv(h, w_vmem, qkv_ref):
    for c in range(w_vmem.shape[0]):
        qkv_ref[c] = dot(h, w_vmem[c]).astype(jnp.bfloat16)


def qkv_kernel(x_ref, gain_ref, bias_ref, w_hbm, qkv_ref, w_vmem, sem):
    first = pl.program_id(0) == 0

    @pl.when(first)
    def _():
        start_qkv_copies(w_hbm, w_vmem, sem)

    h = layer_norm(x_ref[...].astype(jnp.float32), gain_ref[...], bias_ref[...])

    @pl.when(first)
    def _():
        wait_qkv_copies(w_hbm, w_vmem, sem)

    project_qkv(h, w_vmem, qkv_ref)


def qkv_call(x, seq, tokens, gain, bias, w_qkv):
    width = x.shape[1]
    offset = seq * tokens // BLOCK_TOKENS
    parts, rows, cols = w_qkv.shape
    chunks = parts * rows // width
    return pl.pallas_call(
        qkv_kernel,
        grid=(tokens // BLOCK_TOKENS,),
        in_specs=[
            pl.BlockSpec((BLOCK_TOKENS, width), lambda i: (offset + i, 0)),
            pl.BlockSpec((1, width), lambda i: (0, 0)),
            pl.BlockSpec((1, width), lambda i: (0, 0)),
            pl.BlockSpec(memory_space=pl.ANY),
        ],
        out_specs=pl.BlockSpec((chunks, BLOCK_TOKENS, cols), lambda i: (0, i, 0)),
        out_shape=jax.ShapeDtypeStruct((chunks, tokens, cols), jnp.bfloat16),
        scratch_shapes=[pltpu.VMEM((chunks, width, cols), jnp.bfloat16), pltpu.SemaphoreType.DMA],
        compiler_params=pltpu.CompilerParams(
            dimension_semantics=('arbitrary',), vmem_limit_bytes=VMEM_LIMIT),
        cost_estimate=cost(2 * tokens * width * chunks * cols, 2 * tokens * (width + chunks * cols) + 2 * width * chunks * cols),
        name='ln_qkv',
    )(x, gain, bias, w_qkv)


def attention_kernel(*refs, head_dim):
    q_ref, k_ref, v_ref = refs[:3]
    o_ref, s_ref, vx_ref = refs[-3:]
    seq_len, pair = q_ref.shape[1:]
    vx_ref[:, :pair] = v_ref[0]
    vx_ref[:, pair:] = jnp.ones((seq_len, pair), jnp.bfloat16)
    low_lane = lax.broadcasted_iota(jnp.int32, (1, pair), 1) < head_dim
    q_pos = lax.broadcasted_iota(jnp.int32, (BLOCK_Q, BLOCK_K), 0)
    k_pos = lax.broadcasted_iota(jnp.int32, (BLOCK_Q, BLOCK_K), 1)
    causal = k_pos <= q_pos
    inv_sqrt = head_dim ** -0.5
    n_blocks = seq_len // BLOCK_Q
    units = [(block, head) for block in range(n_blocks) for head in range(2)]

    def head_query(unit):
        block, head = unit
        q_blk = q_ref[0, block * BLOCK_Q:(block + 1) * BLOCK_Q, :] * jnp.bfloat16(inv_sqrt)
        keep = low_lane if head == 0 else jnp.logical_not(low_lane)
        return jnp.where(keep, q_blk, jnp.zeros_like(q_blk))

    def score_chunk(unit_idx, q_h, c, run_max):
        block, _ = units[unit_idx]
        k_blk = k_ref[0, c * BLOCK_K:(c + 1) * BLOCK_K, :]
        s = lax.dot_general(q_h, k_blk, (((1,), (1,)), ((), ())), preferred_element_type=jnp.float32)
        if c == block:
            s = jnp.where(causal, s, -jnp.inf)
        s_ref[unit_idx % 2, :, c * BLOCK_K:(c + 1) * BLOCK_K] = s
        chunk_max = s[:, :128]
        for j in range(1, BLOCK_K // 128):
            chunk_max = jnp.maximum(chunk_max, s[:, j * 128:(j + 1) * 128])
        return chunk_max if run_max is None else jnp.maximum(run_max, chunk_max)

    def value_chunk(unit_idx, row_max, c):
        s = s_ref[unit_idx % 2, :, c * BLOCK_K:(c + 1) * BLOCK_K]
        p = jnp.exp2((s - row_max) * LOG2_E).astype(jnp.bfloat16)
        return dot(p, vx_ref[c * BLOCK_K:(c + 1) * BLOCK_K, :])

    run_max = None
    row_max = None
    held = None
    for step in range(len(units) + 1):
        n_score = units[step][0] + 1 if step < len(units) else 0
        n_value = units[step - 1][0] + 1 if step > 0 else 0
        if step > 0:
            row_max = jnp.max(run_max, axis=1, keepdims=True)
        run_max = None
        acc = None
        q_h = head_query(units[step]) if n_score else None
        for c in range(max(n_score, n_value)):
            if c < n_score:
                run_max = score_chunk(step, q_h, c, run_max)
            if c < n_value:
                part = value_chunk(step - 1, row_max, c)
                acc = part if acc is None else acc + part
        if n_value:
            block, head = units[step - 1]
            out = acc[:, :pair] / acc[:, pair:]
            if head == 0:
                held = out
            else:
                o_ref[block * BLOCK_Q:(block + 1) * BLOCK_Q, :] = jnp.where(low_lane, held, out).astype(jnp.bfloat16)


def attention_call(qkv, qkv_seq, seq, batch, seq_len, head_dim, buffer):
    chunks, _, cols = qkv.shape
    pair = 2 * head_dim
    subs = cols // 3 // pair
    spec = lambda t: pl.BlockSpec((1, seq_len, pair), lambda g: (g // subs, qkv_seq, t * subs + g % subs))
    held = [] if buffer is None else [buffer]
    return pl.pallas_call(
        functools.partial(attention_kernel, head_dim=head_dim),
        grid=(chunks * subs,),
        in_specs=[spec(0), spec(1), spec(2)] + [pl.BlockSpec(memory_space=pl.ANY) for _ in held],
        out_specs=pl.BlockSpec((seq_len, pair), lambda g: (seq, g)),
        out_shape=jax.ShapeDtypeStruct((batch * seq_len, chunks * subs * pair), jnp.bfloat16),
        input_output_aliases={3: 0} if held else {},
        scratch_shapes=[pltpu.VMEM((2, BLOCK_Q, seq_len), jnp.float32), pltpu.VMEM((seq_len, 2 * pair), jnp.bfloat16)],
        compiler_params=pltpu.CompilerParams(
            dimension_semantics=('arbitrary',), vmem_limit_bytes=VMEM_LIMIT),
        cost_estimate=cost(9 * seq_len * seq_len * chunks * cols // 4, 2 * seq_len * chunks * (cols + subs * pair)),
        name='causal_attention',
    )(qkv, qkv, qkv, *held)


def ffn_body(first, r_ref, o_ref, gain_ref, bias_ref, bsum_ref, bup_ref, wout_hbm, wup_hbm, wdown_hbm,
             acc_ref, wout_vmem, wup_vmem, wdown_vmem, sems):
    parts = wup_vmem.shape[0]
    early = 2
    out_rows = wout_hbm.shape[1]
    early_copies = []
    for i in range(parts):
        pos = (i % TP_SIZE) * (parts // TP_SIZE) + i // TP_SIZE
        early_copies.append(pltpu.make_async_copy(wout_hbm.at[i], wout_vmem.at[pl.ds(pos * out_rows, out_rows)], sems.at[0]))
    late_copies = []
    for lo, hi, sem, group in ((0, early, 0, early_copies), (early, parts, 1, late_copies)):
        for src, dst in ((wup_hbm, wup_vmem), (wdown_hbm, wdown_vmem)):
            group.append(pltpu.make_async_copy(src.at[pl.ds(lo, hi - lo)], dst.at[pl.ds(lo, hi - lo)], sems.at[sem]))

    @pl.when(first)
    def _():
        for cp in early_copies + late_copies:
            cp.start()

    h = layer_norm(r_ref[...].astype(jnp.float32), gain_ref[...], bias_ref[...])

    def wait_all(copies):
        @pl.when(first)
        def _():
            for cp in copies:
                cp.wait()

    wait_all(early_copies)
    acc_ref[...] = dot(o_ref[...], wout_vmem[...]) + bsum_ref[...]
    hidden = dot(h, wup_vmem[0]) + bup_ref[0]
    for c in range(parts):
        if c + 1 == early:
            wait_all(late_copies)
        ahead = dot(h, wup_vmem[c + 1]) + bup_ref[c + 1] if c + 1 < parts else None
        gelu_out = gelu_tanh(hidden).astype(jnp.bfloat16)
        acc_ref[...] += dot(gelu_out, wdown_vmem[c])
        hidden = ahead
    return r_ref[...].astype(jnp.float32) + acc_ref[...]


def mid_kernel(r_ref, o_ref, gain_ref, bias_ref, bsum_ref, bup_ref, ngain_ref, nbias_ref, wout_hbm, wup_hbm, wdown_hbm,
               wqkv_hbm, res_ref, qkv_ref, acc_ref, wout_vmem, wup_vmem, wdown_vmem, wqkv_vmem, sems):
    first = pl.program_id(0) == 0

    @pl.when(first)
    def _():
        start_qkv_copies(wqkv_hbm, wqkv_vmem, sems.at[2])

    r_new = ffn_body(first, r_ref, o_ref, gain_ref, bias_ref, bsum_ref, bup_ref, wout_hbm, wup_hbm, wdown_hbm,
                     acc_ref, wout_vmem, wup_vmem, wdown_vmem, sems)
    res_ref[...] = r_new
    h_next = layer_norm(r_new, ngain_ref[...], nbias_ref[...])

    @pl.when(first)
    def _():
        wait_qkv_copies(wqkv_hbm, wqkv_vmem, sems.at[2])

    project_qkv(h_next, wqkv_vmem, qkv_ref)


def last_kernel(rows_ref, r_ref, o_ref, gain_ref, bias_ref, bsum_ref, bup_ref, wout_hbm, wup_hbm, wdown_hbm,
                y_ref, acc_ref, wout_vmem, wup_vmem, wdown_vmem, sems):
    first = pl.program_id(0) == 0
    y_ref[...] = ffn_body(first, r_ref, o_ref, gain_ref, bias_ref, bsum_ref, bup_ref, wout_hbm, wup_hbm, wdown_hbm,
                          acc_ref, wout_vmem, wup_vmem, wdown_vmem, sems).astype(jnp.bfloat16)


def mid_call(r, o, gain, bias, bsum, bup, ngain, nbias, w_out, w_up, w_down, w_qkv):
    tokens, width = r.shape
    parts, rows, cols = w_qkv.shape
    chunks = parts * rows // width
    row = pl.BlockSpec((BLOCK_TOKENS, width), lambda i: (i, 0))
    vec = pl.BlockSpec((1, width), lambda i: (0, 0))
    bup_spec = pl.BlockSpec(bup.shape, lambda i: (0, 0, 0))
    hbm = pl.BlockSpec(memory_space=pl.ANY)
    return pl.pallas_call(
        mid_kernel,
        grid=(tokens // BLOCK_TOKENS,),
        in_specs=[row, row, vec, vec, vec, bup_spec, vec, vec, hbm, hbm, hbm, hbm],
        out_specs=[row, pl.BlockSpec((chunks, BLOCK_TOKENS, cols), lambda i: (0, i, 0))],
        out_shape=[jax.ShapeDtypeStruct((tokens, width), jnp.float32),
                   jax.ShapeDtypeStruct((chunks, tokens, cols), jnp.bfloat16)],
        scratch_shapes=[pltpu.VMEM((BLOCK_TOKENS, width), jnp.float32), pltpu.VMEM((width, width), jnp.bfloat16),
                        pltpu.VMEM(w_up.shape, jnp.bfloat16), pltpu.VMEM(w_down.shape, jnp.bfloat16),
                        pltpu.VMEM((chunks, width, cols), jnp.bfloat16), pltpu.SemaphoreType.DMA((3,))],
        compiler_params=pltpu.CompilerParams(
            dimension_semantics=('arbitrary',), vmem_limit_bytes=VMEM_LIMIT),
        cost_estimate=cost(24 * tokens * width * width, 20 * tokens * width),
        name='ffn_qkv',
    )(r, o, gain, bias, bsum, bup, ngain, nbias, w_out, w_up, w_down, w_qkv)


def last_call(r, o, gain, bias, bsum, bup, w_out, w_up, w_down, start, blocks, blk):
    width = r.shape[1]
    count = blocks.shape[0] * blk
    per = blk // BLOCK_TOKENS
    offset = start // BLOCK_TOKENS
    row = pl.BlockSpec((BLOCK_TOKENS, width), lambda i, rows: (offset + rows[i // per] * per + i % per, 0))
    vec = pl.BlockSpec((1, width), lambda i, rows: (0, 0))
    hbm = pl.BlockSpec(memory_space=pl.ANY)
    return pl.pallas_call(
        last_kernel,
        grid_spec=pltpu.PrefetchScalarGridSpec(
            num_scalar_prefetch=1,
            grid=(count // BLOCK_TOKENS,),
            in_specs=[row, pl.BlockSpec((BLOCK_TOKENS, width), lambda i, rows: (rows[i // per] * per + i % per, 0)),
                      vec, vec, vec, pl.BlockSpec(bup.shape, lambda i, rows: (0, 0, 0)), hbm, hbm, hbm],
            out_specs=pl.BlockSpec((BLOCK_TOKENS, width), lambda i, rows: (i, 0)),
            scratch_shapes=[pltpu.VMEM((BLOCK_TOKENS, width), jnp.float32), pltpu.VMEM((width, width), jnp.bfloat16),
                            pltpu.VMEM(w_up.shape, jnp.bfloat16), pltpu.VMEM(w_down.shape, jnp.bfloat16),
                            pltpu.SemaphoreType.DMA((2,))]),
        out_shape=jax.ShapeDtypeStruct((count, width), jnp.bfloat16),
        compiler_params=pltpu.CompilerParams(
            dimension_semantics=('arbitrary',), vmem_limit_bytes=VMEM_LIMIT),
        cost_estimate=cost(18 * count * width * width, 8 * count * width),
        name='ffn_out',
    )(blocks, r, o, gain, bias, bsum, bup, w_out, w_up, w_down)


def solution(mesh):
    tp_size = mesh.shape['tp']
    dp_size = mesh.shape['dp']
    act_spec = P('dp', 'tp', None)

    def local_fn(x_in, ln_gain, ln_bias, w_qkv, w_out, b_out, w_up, b_up, w_down, b_down):
        n_layers, width, _, heads, head_dim = w_qkv.shape
        dp_idx = lax.axis_index('dp')
        tp_idx = lax.axis_index('tp')
        batch_all, blk, _ = x_in.shape
        batch = batch_all // tp_size
        seq_len = blk * tp_size
        tokens = batch * seq_len

        def gather(shard):
            return lax.all_gather(shard, ('dp', 'tp'), axis=0, tiled=False)

        def half(arr, axis):
            size = arr.shape[axis] // dp_size
            return lax.dynamic_slice_in_dim(arr, dp_idx * size, size, axis)

        def qkv_shard(layer):
            return half(w_qkv[layer].reshape(width, 3 * heads * head_dim), 0)

        def ffn_shards(layer):
            return half(w_out[layer].reshape(heads * head_dim, width), 0), half(w_up[layer], 1), half(w_down[layer], 0)

        def exchange(pieces):
            return [piece if k == 0 else lax.ppermute(piece, 'tp', [(i, i ^ k) for i in range(tp_size)])
                    for k, piece in pieces]

        def ffn_weights(shards):
            return tuple(gather(shard) for shard in shards)

        bup_all = lax.all_gather(half(b_up, 1), ('dp', 'tp'), axis=1, tiled=False)
        bsum = b_out + b_down
        peers = [jnp.bitwise_xor(tp_idx, k) for k in range(tp_size)]
        far_first = [k for k in reversed(range(tp_size))]

        x_parts = x_in.reshape(tp_size, batch, blk, width)
        x_send = [[lax.dynamic_slice(x_parts, (peers[k], b, 0, 0), (1, 1, blk, width)) for k in far_first]
                  for b in range(batch)]
        x_all = jnp.zeros((batch, tp_size, blk, width), jnp.bfloat16)

        def place(x_all, b, received):
            for k, piece in zip(far_first, received):
                x_all = lax.dynamic_update_slice(x_all, piece, (b, peers[k], 0, 0))
            return x_all

        received = exchange(list(zip(far_first, x_send[0])))
        first_shard = qkv_shard(0)
        qkv_w = gather(first_shard)
        _, received = lax.optimization_barrier((first_shard, received))
        x_all = place(x_all, 0, received)
        x_all, x_send[1:], shards = lax.optimization_barrier((x_all, x_send[1:], ffn_shards(0)))
        received = [exchange(list(zip(far_first, send))) for send in x_send[1:]]
        weights = [ffn_weights(shards)]

        def norm_args(layer):
            return ln_gain[layer:layer + 1], ln_bias[layer:layer + 1]

        later = [(qkv_shard(layer), ffn_shards(layer)) for layer in range(1, n_layers)]
        qkv = [qkv_call(x_all.reshape(tokens, width), 0, seq_len, *norm_args(0), qkv_w)]
        attn = attention_call(qkv[0], 0, 0, batch, seq_len, head_dim, None)
        for b in range(1, batch):
            x_all, got, attn, later = lax.optimization_barrier((x_all, received[b - 1], attn, later))
            x_all = place(x_all, b, got)
            qkv.append(qkv_call(x_all.reshape(tokens, width), b, seq_len, *norm_args(0), qkv_w))
            attn = attention_call(qkv[b], 0, b, batch, seq_len, head_dim, attn)
        later_qkv = []
        for layer, (qkv_part, ffn_part) in enumerate(later):
            later_qkv.append(gather(qkv_part))
            weights.append(ffn_weights(ffn_part))

        def args(layer):
            return (*norm_args(layer), bsum[layer:layer + 1], bup_all[layer][:, None, :])

        residual = x_all.reshape(tokens, width)
        for layer in range(n_layers - 1):
            if layer:
                attn = None
                for b in range(batch):
                    attn = attention_call(qkv_all, b, b, batch, seq_len, head_dim, attn)
            residual, qkv_all = mid_call(residual, attn, *args(layer), *norm_args(layer + 1), *weights[layer],
                                         later_qkv[layer])
        layer = n_layers - 1
        y_out = jnp.zeros((tp_size, batch, blk, width), jnp.bfloat16)
        sent = []
        done = None
        for b in range(batch):
            if done is not None:
                qkv_all, done = lax.optimization_barrier((qkv_all, done))
            attn = attention_call(qkv_all, b, 0, 1, seq_len, head_dim, None)
            groups = [far_first] if b + 1 < batch else [far_first[:tp_size // 2], far_first[tp_size // 2:]]
            done = None
            for group in groups:
                order = jnp.stack([peers[k] for k in group]).astype(jnp.int32)
                if done is not None:
                    order, done = lax.optimization_barrier((order, done))
                    sent[-1] = (sent[-1][0], done, sent[-1][2])
                done = last_call(residual, attn, *args(layer), *weights[layer], b * seq_len, order, blk)
                sent.append((b, done, group))
        for b, y, group in sent:
            y = y.reshape(len(group), 1, 1, blk, width)
            for k, piece in zip(group, exchange([(k, y[i]) for i, k in enumerate(group)])):
                y_out = lax.dynamic_update_slice(y_out, piece, (peers[k], b, 0, 0))
        return y_out.reshape(batch_all, blk, width)

    in_specs = (act_spec, P(), P(), P(None, None, None, 'tp', None), P(None, 'tp', None, None), P(),
                P(None, None, 'tp'), P(None, 'tp'), P(None, 'tp', None), P())
    return jax.shard_map(local_fn, mesh=mesh, in_specs=in_specs, out_specs=act_spec, check_vma=False)
```

time: 2720 us -> 738 us (0.27)
  matrix products: 1270 us -> 0 us
  waiting for transfers between devices: 763 us -> 127 us
  Pallas kernels: 0 us -> 509 us
  blocking collectives: 382 us -> 10.1 us
  other arithmetic: 122 us -> 1.21 us
  local copies, waits for them, and re-layouts: 133 us -> 62.6 us
    dot_general x24 -> x0, matrix products: 789 us -> none  [the longest x16 429 us: one_block(): jnp.einsum('bhqk,bkhe->bqhe', attn_prob, values, preferred_element_type=j...]
    pallas_call x0 -> x10, Pallas kernels: none -> 509 us  [the longest x4 212 us: attention_call(): pl.pallas_call(functools.partial(attention_kernel, head_dim=head_dim), gr...]
    sub x16 -> x0, matrix products: 486 us -> none  [one_block(): attn_prob = jax.nn.softmax(scores, axis=-1).astype(jnp.bfloat16)]
    all_gather x2 -> x8, waiting for transfers between devices: 401 us -> 10.1 us  [gather(): return lax.all_gather(shard, ('dp', 'tp'), axis=0, tiled=False)]
    all_to_all x1 -> x0, blocking collectives: 382 us -> none  [layer(): lax.all_to_all(partial.astype(jnp.bfloat16), 'tp', 1, 1, tiled=True)]
    all_to_all x1 -> x0, waiting for transfers between devices: 362 us -> none  [layer(): lax.all_to_all(partial.astype(jnp.bfloat16), 'tp', 1, 1, tiled=True)]
    ppermute x0 -> x12, waiting for transfers between devices: none -> 114 us  [exchange(): lax.ppermute(piece, 'tp', [(i, i ^ k) for i in range(tp_size)])]
    reduce_sum x6 -> x0, other arithmetic: 79.7 us -> none  [the longest x2 44 us: layer(): jnp.sum(received.reshape(batch, tp_size, seq_len // tp_size, width), axis...]
  transfers between devices with their start and end apart: 3 -> 20, of which waited for: 3 -> 7; matrix products, arithmetic and copies ran while one was open for 0% -> 7% of each run, Pallas kernels for 0% -> 50%
where the time goes in v1:
time: 738 us; the launch traced here: 733 us
  Pallas kernels  509 us (69%)
  waiting for transfers between devices  127 us (17%)
  local copies, waits for them, and re-layouts  62.6 us (8%)
  between operations  14 us (2%)
  starting transfers between devices  10.2 us (1%)
  blocking collectives  10.1 us (1%)
    pallas_call x4, Pallas kernels, attention_call(): pl.pallas_call(functools.partial(attention_kernel, head_dim=head_dim), gr...  212 us
    pallas_call x1, Pallas kernels, mid_call(): pl.pallas_call(mid_kernel, grid=(tokens // BLOCK_TOKENS,), in_specs=[row,...  137 us
    pallas_call x3, Pallas kernels, last_call(): pl.pallas_call(last_kernel, grid_spec=pltpu.PrefetchScalarGridSpec(num_sc...  116 us
    ppermute x12, waiting for transfers between devices, exchange(): lax.ppermute(piece, 'tp', [(i, i ^ k) for i in range(tp_size)])  114 us
    pallas_call x2, Pallas kernels, qkv_call(): pl.pallas_call(qkv_kernel, grid=(tokens // BLOCK_TOKENS,), in_specs=[pl.B...  43.6 us
  transfers between devices with their start and end apart: 20, of which 7 were waited for; matrix products, arithmetic and copies ran while one was open for 7% of the time, Pallas kernels for 50%

profile of v1, /device:TPU:0, one launch (start us, length us, event | category | flops | bytes accessed | tf_op | source)
XLA Modules:
  0.0 733.4 jit_solution(12112867217517169982)
XLA Ops:
  6.5 3.5 fusion.4
  10.1 1.2 copy.14
  11.4 6.6 constant_dynamic-slice_fusion.4
  18.0 2.7 collective-permute-start
  20.7 0.6 collective-permute-start.1
  21.4 0.9 fusion.5
  22.3 0.7 constant_dynamic-slice_fusion.3
  23.0 2.7 fusion.2
  25.7 1.1 dynamic-slice_bitcast_fusion.2
  26.7 4.0 fusion.3
  30.7 1.1 dynamic-slice_bitcast_fusion.3
  31.8 30.4 %collective-permute-done = bf16[1,1,512,1024]{3,2,1,0:T(8,128)(2,1)} collective-permute-done((bf16[1,1,512,1024]{3,2,1,0:T(8,128)(2,1)}, bf16[1,1,512,1024]{3,2,1,0:T(8,128)(2,1)}, u32[]{:S(2)}, u32[]{:S(2)}) %collective-permute-start) | collective-permute-done | bytes 1048608 | tf_op jit(solution)/shard_map/ppermute | solution.py:335
  62.2 29.8 %collective-permute-done.1 = bf16[1,1,512,1024]{3,2,1,0:T(8,128)(2,1)} collective-permute-done((bf16[1,1,512,1024]{3,2,1,0:T(8,128)(2,1)}, bf16[1,1,512,1024]{3,2,1,0:T(8,128)(2,1)}, u32[]{:S(2)}, u32[]{:S(2)}) %collective-permute-start.1) | collective-permute-done | bytes 1048608 | tf_op jit(solution)/shard_map/ppermute | solution.py:335
  92.1 4.5 broadcast_in_dim.7
  96.5 2.3 constant_dynamic-update-slice_fusion.13
  98.8 2.3 constant_dynamic-update-slice_fusion.12
  101.1 2.3 constant_dynamic-update-slice_fusion.11
  103.4 1.0 constant_dynamic-update-slice_fusion.10
  104.5 0.7 all-gather.22.cloned.1.call-update
  105.2 0.5 all-gather.24.cloned.1.call-update
  105.7 0.6 all-gather.26.cloned.1.call-start
  106.3 2.1 constant_dynamic-slice_fusion.2
  108.4 2.3 copy.15
  110.7 1.7 constant_dynamic-slice_fusion.1
  112.4 1.1 dynamic-slice_bitcast_fusion
  113.5 2.3 dynamic-slice_bitcast_fusion.1
  115.8 0.6 fusion.8
  116.5 1.4 collective-permute-start.4
  117.9 0.4 collective-permute-start.5
  118.3 21.8 %ln_qkv.2.refs_0_.refs_1_.refs_2_ = bf16[4,2048,768]{2,1,0:T(8,128)(2,1)} custom-call(bf16[4096,1024]{1,0:T(8,128)(2,1)} %bitcast.9.x_ref, f32[1,1024]{1,0:T(1,128)} %get-tuple-element.90.gain_ref, f32[1,1024]{1,0:T(1,128)} %get-tuple-element.85.bias_ref, bf16[8,512,768]{2,1,0:T(8,128)(2,1)} %bitcast.67), custom_call_target="tpu_custom_call" | custom-call | flops 12884901888 | bytes 23068672 | tf_op jit(solution)/shard_map/ln_qkv/pallas_call | solution.py:85
  140.1 53.2 %causal_attention.4.refs_3_ = bf16[4096,1024]{1,0:T(8,128)(2,1)} custom-call(bf16[4,2048,768]{2,1,0:T(8,128)(2,1)} %ln_qkv.2.refs_0_.refs_1_.refs_2_, bf16[4,2048,768]{2,1,0:T(8,128)(2,1)} %ln_qkv.2.refs_0_.refs_1_.refs_2_, bf16[4,2048,768]{2,1,0:T(8,128)(2,1)} %ln_qkv.2.refs_0_.refs_1_.refs_2_), custom_call_target="tpu_custom_call" | custom-call | flops 28991029248 | bytes 16777216 | tf_op jit(solution)/shard_map/causal_attention/pallas_call | solution.py:173
  193.5 0.5 all-gather.28.cloned.1.call-update
  194.0 0.7 all-gather.30.cloned.1.call-update
  194.8 10.1 %all-gather.1 = f32[2,4096]{1,0:T(2,128)S(1)} all-gather(f32[2,512]{1,0:T(2,128)S(1)} %constant_dynamic-slice_fusion), channel_id=3, replica_groups=mesh['dp'=2,'tp'=4] {'dp','tp'}, dimensions={1}, use_global_device_ids=true | all-gather | bytes 36864 | tf_op jit(solution)/shard_map/all_gather | solution.py:341
  204.9 0.6 pad_add_fusion.rows_ref
  205.5 0.6 pad_add_fusion.1
  206.1 0.6 fusion.7
  206.7 0.6 fusion.6
  207.4 1.0 constant_dynamic-update-slice_fusion.9
  208.4 1.0 constant_dynamic-update-slice_fusion.8
  209.5 2.3 constant_dynamic-update-slice_fusion.7
  211.7 1.0 constant_dynamic-update-slice_fusion.6
  212.8 21.8 %ln_qkv.3.refs_0_.refs_1_.refs_2_ = bf16[4,2048,768]{2,1,0:T(8,128)(2,1)} custom-call(bf16[4096,1024]{1,0:T(8,128)(2,1)} %bitcast.15.x_ref.r_ref, f32[1,1024]{1,0:T(1,128)} %get-tuple-element.90.gain_ref, f32[1,1024]{1,0:T(1,128)} %get-tuple-element.85.bias_ref, bf16[8,512,768]{2,1,0:T(8,128)(2,1)} %bitcast.68), custom_call_target="tpu_custom_call" | custom-call | flops 12884901888 | bytes 23068672 | tf_op jit(solution)/shard_map/ln_qkv/pallas_call | solution.py:85
  234.6 52.9 %causal_attention.5.o_ref = bf16[4096,1024]{1,0:T(8,128)(2,1)} custom-call(bf16[4,2048,768]{2,1,0:T(8,128)(2,1)} %ln_qkv.3.refs_0_.refs_1_.refs_2_, bf16[4,2048,768]{2,1,0:T(8,128)(2,1)} %ln_qkv.3.refs_0_.refs_1_.refs_2_, bf16[4,2048,768]{2,1,0:T(8,128)(2,1)} %ln_qkv.3.refs_0_.refs_1_.refs_2_, ...), custom_call_target="tpu_custom_call", output_to_operand_aliasing={{}: (3, {})} | custom-call | flops 28991029248 | bytes 16777216 | tf_op jit(solution)/shard_map/causal_attention/pallas_call | solution.py:173
  287.6 10.1 %all-gather.26.cloned.1.call-done = bf16[4096,768]{1,0:T(8,128)(2,1)} async-done(((bf16[512,768]{1,0:T(8,128)(2,1)}), bf16[4096,768]{1,0:T(8,128)(2,1)}) %all-gather.26.cloned.1.call-update) | async-done | bytes 6291472 | tf_op jit(solution)/shard_map/all_gather | solution.py:322
  297.7 136.9 %ffn_qkv.1 = (f32[4096,1024]{1,0:T(8,128)}, bf16[4,4096,768]{2,1,0:T(8,128)(2,1)}) custom-call(bf16[4096,1024]{1,0:T(8,128)(2,1)} %bitcast.15.x_ref.r_ref, bf16[4096,1024]{1,0:T(8,128)(2,1)} %causal_attention.5.o_ref, f32[1,1024]{1,0:T(1,128)} %get-tuple-element.90.gain_ref, f32[1,1024]{1,0:T(1,128)} %get-tuple-element.85.bias_ref, ...), custom_call_target="tpu_custom_call" | custom-call | flops 103079215104 | bytes 83886080 | tf_op jit(solution)/shard_map/ffn_qkv/pallas_call | solution.py:263
  434.5 52.9 %causal_attention.6.o_ref = bf16[2048,1024]{1,0:T(8,128)(2,1)} custom-call(bf16[4,4096,768]{2,1,0:T(8,128)(2,1)} %get-tuple-element.56.refs_0_.refs_1_.refs_2_, bf16[4,4096,768]{2,1,0:T(8,128)(2,1)} %get-tuple-element.56.refs_0_.refs_1_.refs_2_, bf16[4,4096,768]{2,1,0:T(8,128)(2,1)} %get-tuple-element.56.refs_0_.refs_1_.refs_2_), custom_call_target="tpu_custom_call" | custom-call | flops 28991029248 | bytes 16777216 | tf_op jit(solution)/shard_map/causal_attention/pallas_call | solution.py:173
  487.5 54.4 %ffn_out.3 = bf16[2048,1024]{1,0:T(8,128)(2,1)} custom-call(s32[4]{0:T(128)} %pad_add_fusion.rows_ref, f32[4096,1024]{1,0:T(8,128)} %get-tuple-element.51.r_ref, bf16[2048,1024]{1,0:T(8,128)(2,1)} %causal_attention.6.o_ref, f32[1,1024]{1,0:T(1,128)} %get-tuple-element.91.ngain_ref.gain_ref, f32[1,1024]{1,0:T(1,128)} %get-tuple-element.84.nbias_ref.bias_ref, ...), custom_call_target="tpu_custom_call" | custom-call | flops 38654705664 | bytes 16777216 | tf_op jit(solution)/shard_map/ffn_out/pallas_call | solution.py:288
  541.8 3.7 slice_bitcast_fusion.3
  545.5 53.1 %causal_attention.7.o_ref = bf16[2048,1024]{1,0:T(8,128)(2,1)} custom-call(bf16[4,4096,768]{2,1,0:T(8,128)(2,1)} %get-tuple-element.56.refs_0_.refs_1_.refs_2_, bf16[4,4096,768]{2,1,0:T(8,128)(2,1)} %get-tuple-element.56.refs_0_.refs_1_.refs_2_, bf16[4,4096,768]{2,1,0:T(8,128)(2,1)} %get-tuple-element.56.refs_0_.refs_1_.refs_2_), custom_call_target="tpu_custom_call" | custom-call | flops 28991029248 | bytes 16777216 | tf_op jit(solution)/shard_map/causal_attention/pallas_call | solution.py:173
  598.6 30.8 %ffn_out.4 = bf16[1024,1024]{1,0:T(8,128)(2,1)} custom-call(s32[2]{0:T(128)} %get-tuple-element.89.rows_ref, f32[4096,1024]{1,0:T(8,128)} %get-tuple-element.51.r_ref, bf16[2048,1024]{1,0:T(8,128)(2,1)} %causal_attention.7.o_ref, f32[1,1024]{1,0:T(1,128)} %get-tuple-element.91.ngain_ref.gain_ref, f32[1,1024]{1,0:T(1,128)} %get-tuple-element.84.nbias_ref.bias_ref, ...), custom_call_target="tpu_custom_call" | custom-call | flops 19327352832 | bytes 8388608 | tf_op jit(solution)/shard_map/ffn_out/pallas_call | solution.py:288
  629.5 1.3 collective-permute-start.6
  630.8 0.6 collective-permute-start.7
  631.4 30.8 %ffn_out.5 = bf16[1024,1024]{1,0:T(8,128)(2,1)} custom-call(s32[2]{0:T(128)} %get-tuple-element.58.rows_ref, f32[4096,1024]{1,0:T(8,128)} %get-tuple-element.51.r_ref, bf16[2048,1024]{1,0:T(8,128)(2,1)} %causal_attention.7.o_ref, f32[1,1024]{1,0:T(1,128)} %get-tuple-element.91.ngain_ref.gain_ref, f32[1,1024]{1,0:T(1,128)} %get-tuple-element.84.nbias_ref.bias_ref, ...), custom_call_target="tpu_custom_call" | custom-call | flops 19327352832 | bytes 8388608 | tf_op jit(solution)/shard_map/ffn_out/pallas_call | solution.py:288
  662.2 0.2 slice_bitcast_fusion.6
  662.4 1.6 collective-permute-start.9
  663.9 0.6 collective-permute-start.10
  664.5 1.3 slice_bitcast_fusion.1
  665.9 1.1 broadcast_in_dim.6
  667.1 11.0 %collective-permute-done.7 = bf16[1,1,512,1024]{3,2,1,0:T(8,128)(2,1)S(1)} collective-permute-done((bf16[1,1,512,1024]{3,2,1,0:T(8,128)(2,1)}, bf16[1,1,512,1024]{3,2,1,0:T(8,128)(2,1)S(1)}, u32[]{:S(2)}, u32[]{:S(2)}) %collective-permute-start.7) | collective-permute-done | bytes 1048608 | tf_op jit(solution)/shard_map/ppermute | solution.py:335
  678.3 1.3 fusion.1
  679.7 20.0 %collective-permute-done.9 = bf16[1,1,512,1024]{3,2,1,0:T(8,128)(2,1)S(1)} collective-permute-done((bf16[1,1,512,1024]{3,2,1,0:T(8,128)(2,1)S(1)}, bf16[1,1,512,1024]{3,2,1,0:T(8,128)(2,1)S(1)}, u32[]{:S(2)}, u32[]{:S(2)}) %collective-permute-start.9) | collective-permute-done | bytes 1048608 | tf_op jit(solution)/shard_map/ppermute | solution.py:335
  699.8 22.8 %collective-permute-done.10 = bf16[1,1,512,1024]{3,2,1,0:T(8,128)(2,1)S(1)} collective-permute-done((bf16[1,1,512,1024]{3,2,1,0:T(8,128)(2,1)S(1)}, bf16[1,1,512,1024]{3,2,1,0:T(8,128)(2,1)S(1)}, u32[]{:S(2)}, u32[]{:S(2)}) %collective-permute-start.10) | collective-permute-done | bytes 1048608 | tf_op jit(solution)/shard_map/ppermute | solution.py:335
  723.0 3.4 copy-done.2
  (60 shorter events, 1.5 us)
Async XLA Ops:
  6.5 188.3 %copy-start = (f32[2,1024]{1,0:T(2,128)S(1)}, f32[2,1024]{1,0:T(2,128)}, u32[]{:S(2)}) copy-start(f32[2,1024]{1,0:T(2,128)} %param.17) | copy-start | bytes 24580
  6.5 111.8 %all-gather.18.cloned.1.call-start = ((), (), s32[]{:S(2)}) async-start(), calls=%async_computation | async-start | bytes 7077888 | tf_op jit(solution)/shard_map/all_gather | solution.py:322
  11.3 276.3 %all-gather.20.cloned.1.call-start = ((), (), s32[]{:S(2)}) async-start(), calls=%async_computation.1 | async-start | bytes 2359296 | tf_op jit(solution)/shard_map/all_gather | solution.py:322
  11.4 10.0 %copy-start.6 = (bf16[2,4,64,1024]{3,2,1,0:T(8,128)(2,1)S(1)}, bf16[2,4,64,1024]{3,2,1,0:T(8,128)(2,1)}, u32[]{:S(2)}) copy-start(bf16[2,4,64,1024]{3,2,1,0:T(8,128)(2,1)} %param.14) | copy-start | bytes 3145732
  18.0 44.3 %collective-permute-start = (bf16[1,1,512,1024]{3,2,1,0:T(8,128)(2,1)}, bf16[1,1,512,1024]{3,2,1,0:T(8,128)(2,1)}, u32[]{:S(2)}, u32[]{:S(2)}) collective-permute-start(bf16[1,1,512,1024]{3,2,1,0:T(8,128)(2,1)} %get-tuple-element.66), channel_id=1, source_target_pairs={{0,3},{1,2},{2,1},{3,0},{4,7},{5,6},{6,5},{7,4}} | collective-permute-start | bytes 3145736 | tf_op jit(solution)/shard_map/ppermute | solution.py:335
  20.7 71.4 %collective-permute-start.1 = (bf16[1,1,512,1024]{3,2,1,0:T(8,128)(2,1)}, bf16[1,1,512,1024]{3,2,1,0:T(8,128)(2,1)}, u32[]{:S(2)}, u32[]{:S(2)}) collective-permute-start(bf16[1,1,512,1024]{3,2,1,0:T(8,128)(2,1)} %get-tuple-element.65), channel_id=1, source_target_pairs={{0,2},{1,3},{2,0},{3,1},{4,6},{5,7},{6,4},{7,5}} | collective-permute-start | bytes 3145736 | tf_op jit(solution)/shard_map/ppermute | solution.py:335
  21.3 70.8 %collective-permute-start.2 = (bf16[1,1,512,1024]{3,2,1,0:T(8,128)(2,1)}, bf16[1,1,512,1024]{3,2,1,0:T(8,128)(2,1)}, u32[]{:S(2)}, u32[]{:S(2)}) collective-permute-start(bf16[1,1,512,1024]{3,2,1,0:T(8,128)(2,1)} %get-tuple-element.64), channel_id=1, source_target_pairs={{0,1},{1,0},{2,3},{3,2},{4,5},{5,4},{6,7},{7,6}} | collective-permute-start | bytes 3145736 | tf_op jit(solution)/shard_map/ppermute | solution.py:335
  31.8 71.5 %copy-start.3 = (bf16[1,1,512,1024]{3,2,1,0:T(8,128)(2,1)S(1)}, bf16[1,1,512,1024]{3,2,1,0:T(8,128)(2,1)}, u32[]{:S(2)}) copy-start(bf16[1,1,512,1024]{3,2,1,0:T(8,128)(2,1)} %get-tuple-element.35) | copy-start | bytes 3145732
  98.8 17.0 %copy-start.9 = (f32[2,1024]{1,0:T(2,128)S(1)}, f32[2,1024]{1,0:T(2,128)}, u32[]{:S(2)}) copy-start(f32[2,1024]{1,0:T(2,128)} %param.12) | copy-start | bytes 24580
  98.8 17.0 %copy-start.10 = (f32[2,1024]{1,0:T(2,128)S(1)}, f32[2,1024]{1,0:T(2,128)}, u32[]{:S(2)}) copy-start(f32[2,1024]{1,0:T(2,128)} %param.11) | copy-start | bytes 24580
  104.4 183.1 %all-gather.22.cloned.1.call-start = ((), (), s32[]{:S(2)}) async-start(), calls=%async_computation.2 | async-start | bytes 9437184 | tf_op jit(solution)/shard_map/all_gather | solution.py:322
  105.2 182.4 %all-gather.24.cloned.1.call-start = ((), (), s32[]{:S(2)}) async-start(), calls=%async_computation.3 | async-start | bytes 9437184 | tf_op jit(solution)/shard_map/all_gather | solution.py:322
  105.7 191.9 %all-gather.26.cloned.1.call-start = ((), (), s32[]{:S(2)}) async-start(), calls=%async_computation.4 | async-start | bytes 7077888 | tf_op jit(solution)/shard_map/all_gather | solution.py:322
  116.4 76.9 %collective-permute-start.3 = (bf16[1,1,512,1024]{3,2,1,0:T(8,128)(2,1)}, bf16[1,1,512,1024]{3,2,1,0:T(8,128)(2,1)S(1)}, u32[]{:S(2)}, u32[]{:S(2)}) collective-permute-start(bf16[1,1,512,1024]{3,2,1,0:T(8,128)(2,1)} %get-tuple-element.37), channel_id=1, source_target_pairs={{0,3},{1,2},{2,1},{3,0},{4,7},{5,6},{6,5},{7,4}} | collective-permute-start | bytes 3145736 | tf_op jit(solution)/shard_map/ppermute | solution.py:335
  116.5 76.9 %collective-permute-start.4 = (bf16[1,1,512,1024]{3,2,1,0:T(8,128)(2,1)}, bf16[1,1,512,1024]{3,2,1,0:T(8,128)(2,1)S(1)}, u32[]{:S(2)}, u32[]{:S(2)}) collective-permute-start(bf16[1,1,512,1024]{3,2,1,0:T(8,128)(2,1)} %get-tuple-element.38), channel_id=1, source_target_pairs={{0,2},{1,3},{2,0},{3,1},{4,6},{5,7},{6,4},{7,5}} | collective-permute-start | bytes 3145736 | tf_op jit(solution)/shard_map/ppermute | solution.py:335
  117.9 75.5 %collective-permute-start.5 = (bf16[1,1,512,1024]{3,2,1,0:T(8,128)(2,1)}, bf16[1,1,512,1024]{3,2,1,0:T(8,128)(2,1)}, u32[]{:S(2)}, u32[]{:S(2)}) collective-permute-start(bf16[1,1,512,1024]{3,2,1,0:T(8,128)(2,1)} %get-tuple-element.39), channel_id=1, source_target_pairs={{0,1},{1,0},{2,3},{3,2},{4,5},{5,4},{6,7},{7,6}} | collective-permute-start | bytes 3145736 | tf_op jit(solution)/shard_map/ppermute | solution.py:335
  140.1 54.7 %copy-start.7 = (f32[2,1024]{1,0:T(2,128)S(1)}, f32[2,1024]{1,0:T(2,128)}, u32[]{:S(2)}) copy-start(f32[2,1024]{1,0:T(2,128)} %param.15) | copy-start | bytes 24580
  140.1 54.7 %copy-start.8 = (f32[2,1024]{1,0:T(2,128)S(1)}, f32[2,1024]{1,0:T(2,128)}, u32[]{:S(2)}) copy-start(f32[2,1024]{1,0:T(2,128)} %param.19) | copy-start | bytes 24580
  193.4 294.1 %all-gather.28.cloned.1.call-start = ((), (), s32[]{:S(2)}) async-start(), calls=%async_computation.5 | async-start | bytes 2359296 | tf_op jit(solution)/shard_map/all_gather | solution.py:322
  194.0 293.5 %all-gather.30.cloned.1.call-start = ((), (), s32[]{:S(2)}) async-start(), calls=%async_computation.6 | async-start | bytes 9437184 | tf_op jit(solution)/shard_map/all_gather | solution.py:322
  194.7 292.7 %all-gather.32.cloned.1.call-start = ((), (), s32[]{:S(2)}) async-start(), calls=%async_computation.7 | async-start | bytes 9437184 | tf_op jit(solution)/shard_map/all_gather | solution.py:322
  629.5 36.3 %collective-permute-start.6 = (bf16[1,1,512,1024]{3,2,1,0:T(8,128)(2,1)}, bf16[1,1,512,1024]{3,2,1,0:T(8,128)(2,1)S(1)}, u32[]{:S(2)}, u32[]{:S(2)}) collective-permute-start(bf16[1,1,512,1024]{3,2,1,0:T(8,128)(2,1)} %get-tuple-element.69), channel_id=1, source_target_pairs={{0,3},{1,2},{2,1},{3,0},{4,7},{5,6},{6,5},{7,4}} | collective-permute-start | bytes 3145736 | tf_op jit(solution)/shard_map/ppermute | solution.py:335
  630.8 47.3 %collective-permute-start.7 = (bf16[1,1,512,1024]{3,2,1,0:T(8,128)(2,1)}, bf16[1,1,512,1024]{3,2,1,0:T(8,128)(2,1)S(1)}, u32[]{:S(2)}, u32[]{:S(2)}) collective-permute-start(bf16[1,1,512,1024]{3,2,1,0:T(8,128)(2,1)} %get-tuple-element.68), channel_id=1, source_target_pairs={{0,2},{1,3},{2,0},{3,1},{4,6},{5,7},{6,4},{7,5}} | collective-permute-start | bytes 3145736 | tf_op jit(solution)/shard_map/ppermute | solution.py:335
  631.4 30.8 %copy-start.5 = (bf16[1024,1024]{1,0:T(8,128)(2,1)S(1)}, bf16[1024,1024]{1,0:T(8,128)(2,1)}, u32[]{:S(2)}) copy-start(bf16[1024,1024]{1,0:T(8,128)(2,1)} %ffn_out.4) | copy-start | bytes 6291460
  631.4 46.8 %collective-permute-start.8 = (bf16[1,1,512,1024]{3,2,1,0:T(8,128)(2,1)}, bf16[1,1,512,1024]{3,2,1,0:T(8,128)(2,1)S(1)}, u32[]{:S(2)}, u32[]{:S(2)}) collective-permute-start(bf16[1,1,512,1024]{3,2,1,0:T(8,128)(2,1)} %get-tuple-element.67), channel_id=1, source_target_pairs={{0,1},{1,0},{2,3},{3,2},{4,5},{5,4},{6,7},{7,6}} | collective-permute-start | bytes 3145736 | tf_op jit(solution)/shard_map/ppermute | solution.py:335
  662.4 37.3 %collective-permute-start.9 = (bf16[1,1,512,1024]{3,2,1,0:T(8,128)(2,1)S(1)}, bf16[1,1,512,1024]{3,2,1,0:T(8,128)(2,1)S(1)}, u32[]{:S(2)}, u32[]{:S(2)}) collective-permute-start(bf16[1,1,512,1024]{3,2,1,0:T(8,128)(2,1)S(1)} %get-tuple-element.77), channel_id=1, source_target_pairs={{0,3},{1,2},{2,1},{3,0},{4,7},{5,6},{6,5},{7,4}} | collective-permute-start | bytes 3145736 | tf_op jit(solution)/shard_map/ppermute | solution.py:335
  663.9 58.6 %collective-permute-start.10 = (bf16[1,1,512,1024]{3,2,1,0:T(8,128)(2,1)S(1)}, bf16[1,1,512,1024]{3,2,1,0:T(8,128)(2,1)S(1)}, u32[]{:S(2)}, u32[]{:S(2)}) collective-permute-start(bf16[1,1,512,1024]{3,2,1,0:T(8,128)(2,1)S(1)} %get-tuple-element.76), channel_id=1, source_target_pairs={{0,2},{1,3},{2,0},{3,1},{4,6},{5,7},{6,4},{7,5}} | collective-permute-start | bytes 3145736 | tf_op jit(solution)/shard_map/ppermute | solution.py:335
  665.8 56.9 %collective-permute-start.11 = (bf16[1,1,512,1024]{3,2,1,0:T(8,128)(2,1)S(1)}, bf16[1,1,512,1024]{3,2,1,0:T(8,128)(2,1)S(1)}, u32[]{:S(2)}, u32[]{:S(2)}) collective-permute-start(bf16[1,1,512,1024]{3,2,1,0:T(8,128)(2,1)S(1)} %slice_bitcast_fusion.1), channel_id=1, source_target_pairs={{0,1},{1,0},{2,3},{3,2},{4,5},{5,4},{6,7},{7,6}} | collective-permute-start | bytes 3145736 | tf_op jit(solution)/shard_map/ppermute | solution.py:335
  665.9 60.5 %copy-start.1 = (f32[2,1024]{1,0:T(2,128)S(1)}, f32[2,1024]{1,0:T(2,128)}, u32[]{:S(2)}) copy-start(f32[2,1024]{1,0:T(2,128)} %param.17) | copy-start | bytes 24580
  666.9 55.9 %copy-start.4 = (bf16[1024,1024]{1,0:T(8,128)(2,1)S(1)}, bf16[1024,1024]{1,0:T(8,128)(2,1)}, u32[]{:S(2)}) copy-start(bf16[1024,1024]{1,0:T(8,128)(2,1)} %ffn_out.5) | copy-start | bytes 6291460
  723.0 3.4 copy-start.2
Sparse Core Ops, SparseCore 0:
  11.4 66.4 all-gather.17
  104.5 27.8 all-gather.19
  134.3 71.3 all-gather.21
  207.4 48.7 all-gather.23
  257.8 39.8 all-gather.25
  299.3 22.2 all-gather.27
  323.4 48.6 all-gather.29
  374.0 48.6 all-gather.31

commit v2 on v1

--- a/solution.py
+++ b/solution.py
@@ -56,49 +56,71 @@
         pltpu.make_async_copy(w_hbm.at[i], w_vmem.at[chunk, pl.ds(half * rows, rows)], sem).wait()
 
 
-def project_qkv(h, w_vmem, qkv_ref):
+def project_qkv(h, w_vmem, qkv_ref, rows):
     for c in range(w_vmem.shape[0]):
-        qkv_ref[c] = dot(h, w_vmem[c]).astype(jnp.bfloat16)
-
-
-def qkv_kernel(x_ref, gain_ref, bias_ref, w_hbm, qkv_ref, w_vmem, sem):
-    first = pl.program_id(0) == 0
-
-    @pl.when(first)
+        qkv_ref[c, rows, :] = dot(h, w_vmem[c]).astype(jnp.bfloat16)
+
+
+def norm_project(x_of, splits, gain_ref, bias_ref, w_vmem, qkv_ref):
+    for lo, hi in splits:
+        h = layer_norm(x_of(lo, hi), gain_ref[...], bias_ref[...])
+        project_qkv(h, w_vmem, qkv_ref, slice(lo, hi))
+
+
+def qkv_kernel(place_ref, *refs, pieces, seq):
+    piece_refs = refs[:pieces]
+    own_ref, gain_ref, bias_ref, w_hbm = refs[pieces:pieces + 4]
+    qkv_ref, res_ref, x_vmem, w_vmem, sems = refs[-5:]
+    blk = own_ref.shape[1]
+    step = pl.program_id(0)
+
+    @pl.when(step == 0)
     def _():
-        start_qkv_copies(w_hbm, w_vmem, sem)
-
-    h = layer_norm(x_ref[...].astype(jnp.float32), gain_ref[...], bias_ref[...])
-
-    @pl.when(first)
-    def _():
-        wait_qkv_copies(w_hbm, w_vmem, sem)
-
-    project_qkv(h, w_vmem, qkv_ref)
-
-
-def qkv_call(x, seq, tokens, gain, bias, w_qkv):
-    width = x.shape[1]
+        start_qkv_copies(w_hbm, w_vmem, sems.at[0])
+        sources = [ref.at[0, 0] for ref in piece_refs] + [own_ref.at[place_ref[pieces] * place_ref[pieces + 1] + seq]]
+        copies = [pltpu.make_async_copy(src, x_vmem.at[pl.ds(place_ref[n] * blk, blk)], sems.at[1])
+                  for n, src in enumerate(sources)]
+        for cp in copies:
+            cp.start()
+        for cp in copies:
+            cp.wait()
+        wait_qkv_copies(w_hbm, w_vmem, sems.at[0])
+
+    row0 = pl.multiple_of(step * BLOCK_TOKENS, BLOCK_TOKENS)
+    res_ref[...] = x_vmem[pl.ds(row0, BLOCK_TOKENS), :]
+    quarter = BLOCK_TOKENS // 4
+    norm_project(lambda lo, hi: x_vmem[pl.ds(row0 + lo, hi - lo), :].astype(jnp.float32),
+                 ((0, quarter), (quarter, BLOCK_TOKENS)), gain_ref, bias_ref, w_vmem, qkv_ref)
+
+
+def qkv_call(place, received, x_own, seq, batch, gain, bias, w_qkv, buffer):
+    blk, width = x_own.shape[1:]
+    tokens = blk * (len(received) + 1)
     offset = seq * tokens // BLOCK_TOKENS
     parts, rows, cols = w_qkv.shape
     chunks = parts * rows // width
+    hbm = pl.BlockSpec(memory_space=pl.ANY)
+    vec = pl.BlockSpec((1, width), lambda i, place: (0, 0))
+    held = [] if buffer is None else [buffer]
+    n_in = len(received) + 5
     return pl.pallas_call(
-        qkv_kernel,
-        grid=(tokens // BLOCK_TOKENS,),
-        in_specs=[
-            pl.BlockSpec((BLOCK_TOKENS, width), lambda i: (offset + i, 0)),
-            pl.BlockSpec((1, width), lambda i: (0, 0)),
-            pl.BlockSpec((1, width), lambda i: (0, 0)),
-            pl.BlockSpec(memory_space=pl.ANY),
-        ],
-        out_specs=pl.BlockSpec((chunks, BLOCK_TOKENS, cols), lambda i: (0, i, 0)),
-        out_shape=jax.ShapeDtypeStruct((chunks, tokens, cols), jnp.bfloat16),
-        scratch_shapes=[pltpu.VMEM((chunks, width, cols), jnp.bfloat16), pltpu.SemaphoreType.DMA],
+        functools.partial(qkv_kernel, pieces=len(received), seq=seq),
+        grid_spec=pltpu.PrefetchScalarGridSpec(
+            num_scalar_prefetch=1,
+            grid=(tokens // BLOCK_TOKENS,),
+            in_specs=[hbm] * (len(received) + 1) + [vec, vec, hbm] + [hbm for _ in held],
+            out_specs=[pl.BlockSpec((chunks, BLOCK_TOKENS, cols), lambda i, place: (0, i, 0)),
+                       pl.BlockSpec((BLOCK_TOKENS, width), lambda i, place: (offset + i, 0))],
+            scratch_shapes=[pltpu.VMEM((tokens, width), jnp.bfloat16), pltpu.VMEM((chunks, width, cols), jnp.bfloat16),
+                            pltpu.SemaphoreType.DMA((2,))]),
+        out_shape=[jax.ShapeDtypeStruct((chunks, tokens, cols), jnp.bfloat16),
+                   jax.ShapeDtypeStruct((batch * tokens, width), jnp.bfloat16)],
+        input_output_aliases={n_in: 1} if held else {},
         compiler_params=pltpu.CompilerParams(
             dimension_semantics=('arbitrary',), vmem_limit_bytes=VMEM_LIMIT),
         cost_estimate=cost(2 * tokens * width * chunks * cols, 2 * tokens * (width + chunks * cols) + 2 * width * chunks * cols),
         name='ln_qkv',
-    )(x, gain, bias, w_qkv)
+    )(place, *received, x_own, gain, bias, w_qkv, *held)
 
 
 def attention_kernel(*refs, head_dim):
@@ -106,14 +128,19 @@
     o_ref, s_ref, vx_ref = refs[-3:]
     seq_len, pair = q_ref.shape[1:]
     vx_ref[:, :pair] = v_ref[0]
-    vx_ref[:, pair:] = jnp.ones((seq_len, pair), jnp.bfloat16)
+
+    @pl.when(pl.program_id(0) == 0)
+    def _():
+        vx_ref[:, pair:] = jnp.ones((seq_len, pair), jnp.bfloat16)
+
     low_lane = lax.broadcasted_iota(jnp.int32, (1, pair), 1) < head_dim
     q_pos = lax.broadcasted_iota(jnp.int32, (BLOCK_Q, BLOCK_K), 0)
     k_pos = lax.broadcasted_iota(jnp.int32, (BLOCK_Q, BLOCK_K), 1)
     causal = k_pos <= q_pos
     inv_sqrt = head_dim ** -0.5
     n_blocks = seq_len // BLOCK_Q
-    units = [(block, head) for block in range(n_blocks) for head in range(2)]
+    order = list(range(0, n_blocks, 2)) + list(range(1, n_blocks, 2))[::-1]
+    units = [(block, head) for block in order for head in range(2)]
 
     def head_query(unit):
         block, head = unit
@@ -186,7 +213,7 @@
 
 
 def ffn_body(first, r_ref, o_ref, gain_ref, bias_ref, bsum_ref, bup_ref, wout_hbm, wup_hbm, wdown_hbm,
-             acc_ref, wout_vmem, wup_vmem, wdown_vmem, sems):
+             acc_ref, wout_vmem, wup_vmem, wdown_vmem, sems, emit, more_waits=lambda: None):
     parts = wup_vmem.shape[0]
     early = 2
     out_rows = wout_hbm.shape[1]
@@ -203,26 +230,28 @@
     def _():
         for cp in early_copies + late_copies:
             cp.start()
-
+        for cp in early_copies:
+            cp.wait()
+
+    acc_ref[...] = dot(o_ref[...], wout_vmem[...]) + bsum_ref[...]
     h = layer_norm(r_ref[...].astype(jnp.float32), gain_ref[...], bias_ref[...])
-
-    def wait_all(copies):
-        @pl.when(first)
-        def _():
-            for cp in copies:
-                cp.wait()
-
-    wait_all(early_copies)
-    acc_ref[...] = dot(o_ref[...], wout_vmem[...]) + bsum_ref[...]
     hidden = dot(h, wup_vmem[0]) + bup_ref[0]
+    half = BLOCK_TOKENS // 2
     for c in range(parts):
         if c + 1 == early:
-            wait_all(late_copies)
+            @pl.when(first)
+            def _():
+                for cp in late_copies:
+                    cp.wait()
+                more_waits()
         ahead = dot(h, wup_vmem[c + 1]) + bup_ref[c + 1] if c + 1 < parts else None
         gelu_out = gelu_tanh(hidden).astype(jnp.bfloat16)
-        acc_ref[...] += dot(gelu_out, wdown_vmem[c])
+        if c + 1 < parts:
+            acc_ref[...] += dot(gelu_out, wdown_vmem[c])
+        else:
+            for rows in (slice(0, half), slice(half, BLOCK_TOKENS)):
+                emit(rows, r_ref[rows, :].astype(jnp.float32) + (acc_ref[rows, :] + dot(gelu_out[rows, :], wdown_vmem[c])))
         hidden = ahead
-    return r_ref[...].astype(jnp.float32) + acc_ref[...]
 
 
 def mid_kernel(r_ref, o_ref, gain_ref, bias_ref, bsum_ref, bup_ref, ngain_ref, nbias_ref, wout_hbm, wup_hbm, wdown_hbm,
@@ -233,23 +262,28 @@
     def _():
         start_qkv_copies(wqkv_hbm, wqkv_vmem, sems.at[2])
 
-    r_new = ffn_body(first, r_ref, o_ref, gain_ref, bias_ref, bsum_ref, bup_ref, wout_hbm, wup_hbm, wdown_hbm,
-                     acc_ref, wout_vmem, wup_vmem, wdown_vmem, sems)
-    res_ref[...] = r_new
-    h_next = layer_norm(r_new, ngain_ref[...], nbias_ref[...])
-
-    @pl.when(first)
-    def _():
-        wait_qkv_copies(wqkv_hbm, wqkv_vmem, sems.at[2])
-
-    project_qkv(h_next, wqkv_vmem, qkv_ref)
+    rows_done = []
+
+    def emit(rows, r_new):
+        res_ref[rows, :] = r_new
+        rows_done.append((rows, r_new))
+
+    ffn_body(first, r_ref, o_ref, gain_ref, bias_ref, bsum_ref, bup_ref, wout_hbm, wup_hbm, wdown_hbm,
+             acc_ref, wout_vmem, wup_vmem, wdown_vmem, sems, emit,
+             lambda: wait_qkv_copies(wqkv_hbm, wqkv_vmem, sems.at[2]))
+    for rows, r_new in rows_done:
+        project_qkv(layer_norm(r_new, ngain_ref[...], nbias_ref[...]), wqkv_vmem, qkv_ref, rows)
 
 
 def last_kernel(rows_ref, r_ref, o_ref, gain_ref, bias_ref, bsum_ref, bup_ref, wout_hbm, wup_hbm, wdown_hbm,
                 y_ref, acc_ref, wout_vmem, wup_vmem, wdown_vmem, sems):
     first = pl.program_id(0) == 0
-    y_ref[...] = ffn_body(first, r_ref, o_ref, gain_ref, bias_ref, bsum_ref, bup_ref, wout_hbm, wup_hbm, wdown_hbm,
-                          acc_ref, wout_vmem, wup_vmem, wdown_vmem, sems).astype(jnp.bfloat16)
+
+    def emit(rows, r_new):
+        y_ref[rows, :] = r_new.astype(jnp.bfloat16)
+
+    ffn_body(first, r_ref, o_ref, gain_ref, bias_ref, bsum_ref, bup_ref, wout_hbm, wup_hbm, wdown_hbm,
+             acc_ref, wout_vmem, wup_vmem, wdown_vmem, sems, emit)
 
 
 def mid_call(r, o, gain, bias, bsum, bup, ngain, nbias, w_out, w_up, w_down, w_qkv):
@@ -277,12 +311,11 @@
     )(r, o, gain, bias, bsum, bup, ngain, nbias, w_out, w_up, w_down, w_qkv)
 
 
-def last_call(r, o, gain, bias, bsum, bup, w_out, w_up, w_down, start, blocks, blk):
+def last_call(r, o, gain, bias, bsum, bup, w_out, w_up, w_down, blocks, blk):
     width = r.shape[1]
     count = blocks.shape[0] * blk
     per = blk // BLOCK_TOKENS
-    offset = start // BLOCK_TOKENS
-    row = pl.BlockSpec((BLOCK_TOKENS, width), lambda i, rows: (offset + rows[i // per] * per + i % per, 0))
+    row = pl.BlockSpec((BLOCK_TOKENS, width), lambda i, rows: (rows[i // per] * per + i % per, 0))
     vec = pl.BlockSpec((1, width), lambda i, rows: (0, 0))
     hbm = pl.BlockSpec(memory_space=pl.ANY)
     return pl.pallas_call(
@@ -290,7 +323,7 @@
         grid_spec=pltpu.PrefetchScalarGridSpec(
             num_scalar_prefetch=1,
             grid=(count // BLOCK_TOKENS,),
-            in_specs=[row, pl.BlockSpec((BLOCK_TOKENS, width), lambda i, rows: (rows[i // per] * per + i % per, 0)),
+            in_specs=[row, row,
                       vec, vec, vec, pl.BlockSpec(bup.shape, lambda i, rows: (0, 0, 0)), hbm, hbm, hbm],
             out_specs=pl.BlockSpec((BLOCK_TOKENS, width), lambda i, rows: (i, 0)),
             scratch_shapes=[pltpu.VMEM((BLOCK_TOKENS, width), jnp.float32), pltpu.VMEM((width, width), jnp.bfloat16),
@@ -311,25 +344,29 @@
 
     def local_fn(x_in, ln_gain, ln_bias, w_qkv, w_out, b_out, w_up, b_up, w_down, b_down):
         n_layers, width, _, heads, head_dim = w_qkv.shape
+        ffn = w_up.shape[2]
         dp_idx = lax.axis_index('dp')
         tp_idx = lax.axis_index('tp')
         batch_all, blk, _ = x_in.shape
         batch = batch_all // tp_size
         seq_len = blk * tp_size
-        tokens = batch * seq_len
 
         def gather(shard):
             return lax.all_gather(shard, ('dp', 'tp'), axis=0, tiled=False)
 
-        def half(arr, axis):
-            size = arr.shape[axis] // dp_size
-            return lax.dynamic_slice_in_dim(arr, dp_idx * size, size, axis)
-
-        def qkv_shard(layer):
-            return half(w_qkv[layer].reshape(width, 3 * heads * head_dim), 0)
-
-        def ffn_shards(layer):
-            return half(w_out[layer].reshape(heads * head_dim, width), 0), half(w_up[layer], 1), half(w_down[layer], 0)
+        def half(arr, layer, axis):
+            sizes = [1, *arr.shape[1:]]
+            sizes[axis] //= dp_size
+            start = [layer] + [0] * (arr.ndim - 1)
+            start[axis] = dp_idx * sizes[axis]
+            return lax.dynamic_slice(arr, start, sizes)[0]
+
+        def qkv_shard(layer, w_qkv):
+            return half(w_qkv, layer, 1).reshape(width // dp_size, 3 * heads * head_dim)
+
+        def ffn_shards(layer, w_out, w_up, w_down):
+            return (half(w_out, layer, 1).reshape(heads * head_dim // dp_size, width), half(w_up, layer, 2),
+                    half(w_down, layer, 1))
 
         def exchange(pieces):
             return [piece if k == 0 else lax.ppermute(piece, 'tp', [(i, i ^ k) for i in range(tp_size)])
@@ -338,50 +375,49 @@
         def ffn_weights(shards):
             return tuple(gather(shard) for shard in shards)
 
-        bup_all = lax.all_gather(half(b_up, 1), ('dp', 'tp'), axis=1, tiled=False)
         bsum = b_out + b_down
         peers = [jnp.bitwise_xor(tp_idx, k) for k in range(tp_size)]
         far_first = [k for k in reversed(range(tp_size))]
 
         x_parts = x_in.reshape(tp_size, batch, blk, width)
-        x_send = [[lax.dynamic_slice(x_parts, (peers[k], b, 0, 0), (1, 1, blk, width)) for k in far_first]
-                  for b in range(batch)]
-        x_all = jnp.zeros((batch, tp_size, blk, width), jnp.bfloat16)
-
-        def place(x_all, b, received):
-            for k, piece in zip(far_first, received):
-                x_all = lax.dynamic_update_slice(x_all, piece, (b, peers[k], 0, 0))
-            return x_all
-
-        received = exchange(list(zip(far_first, x_send[0])))
-        first_shard = qkv_shard(0)
+        place = jnp.stack([peers[k] for k in far_first] + [jnp.full_like(tp_idx, batch)]).astype(jnp.int32)
+
+        def x_send(parts, b):
+            return [(k, lax.dynamic_slice(parts, (peers[k], b, 0, 0), (1, 1, blk, width))) for k in far_first if k]
+
+        first_shard = qkv_shard(0, w_qkv)
         qkv_w = gather(first_shard)
-        _, received = lax.optimization_barrier((first_shard, received))
-        x_all = place(x_all, 0, received)
-        x_all, x_send[1:], shards = lax.optimization_barrier((x_all, x_send[1:], ffn_shards(0)))
-        received = [exchange(list(zip(far_first, send))) for send in x_send[1:]]
+        received = exchange(x_send(x_parts, 0))
+        biases = exchange([(k, b_up) for k in range(tp_size)])
+        bup_all = jnp.zeros((tp_size, n_layers, ffn), jnp.float32)
+        for k, piece in enumerate(biases):
+            bup_all = lax.dynamic_update_slice(bup_all, piece[None], (peers[k], 0, 0))
+        bup_all = bup_all.reshape(tp_size, n_layers, dp_size, ffn // dp_size).transpose(1, 2, 0, 3)
+        bup_all = bup_all.reshape(n_layers, dp_size * tp_size, 1, ffn // dp_size)
+        first_shard, received, bup_all = lax.optimization_barrier((first_shard, received, bup_all))
+        received, x_later, shards = lax.optimization_barrier((received, x_parts, ffn_shards(0, w_out, w_up, w_down)))
+        pieces = [received] + [exchange(x_send(x_later, b)) for b in range(1, batch)]
         weights = [ffn_weights(shards)]
 
         def norm_args(layer):
             return ln_gain[layer:layer + 1], ln_bias[layer:layer + 1]
 
-        later = [(qkv_shard(layer), ffn_shards(layer)) for layer in range(1, n_layers)]
-        qkv = [qkv_call(x_all.reshape(tokens, width), 0, seq_len, *norm_args(0), qkv_w)]
-        attn = attention_call(qkv[0], 0, 0, batch, seq_len, head_dim, None)
-        for b in range(1, batch):
-            x_all, got, attn, later = lax.optimization_barrier((x_all, received[b - 1], attn, later))
-            x_all = place(x_all, b, got)
-            qkv.append(qkv_call(x_all.reshape(tokens, width), b, seq_len, *norm_args(0), qkv_w))
-            attn = attention_call(qkv[b], 0, b, batch, seq_len, head_dim, attn)
+        qkv, residual, attn = None, None, None
+        params = (w_qkv, w_out, w_up, w_down)
+        for b in range(batch):
+            got = pieces[b]
+            if b:
+                got, attn, params = lax.optimization_barrier((got, attn, params))
+            qkv, residual = qkv_call(place, got, x_in, b, batch, *norm_args(0), qkv_w, residual)
+            attn = attention_call(qkv, 0, b, batch, seq_len, head_dim, attn)
         later_qkv = []
-        for layer, (qkv_part, ffn_part) in enumerate(later):
-            later_qkv.append(gather(qkv_part))
-            weights.append(ffn_weights(ffn_part))
+        for layer in range(1, n_layers):
+            later_qkv.append(gather(qkv_shard(layer, params[0])))
+            weights.append(ffn_weights(ffn_shards(layer, *params[1:])))
 
         def args(layer):
-            return (*norm_args(layer), bsum[layer:layer + 1], bup_all[layer][:, None, :])
-
-        residual = x_all.reshape(tokens, width)
+            return (*norm_args(layer), bsum[layer:layer + 1], bup_all[layer])
+
         for layer in range(n_layers - 1):
             if layer:
                 attn = None
@@ -390,25 +426,31 @@
             residual, qkv_all = mid_call(residual, attn, *args(layer), *norm_args(layer + 1), *weights[layer],
                                          later_qkv[layer])
         layer = n_layers - 1
-        y_out = jnp.zeros((tp_size, batch, blk, width), jnp.bfloat16)
-        sent = []
-        done = None
+        far, near = far_first[:tp_size // 2], far_first[tp_size // 2:]
+        attn, done, sent = None, None, []
+
+        def finish(todo):
+            order = jnp.stack([b * tp_size + peers[k] for b, k in todo]).astype(jnp.int32)
+            if done is not None:
+                order, sent[-1] = lax.optimization_barrier((order, done))
+            y = last_call(residual, attn, *args(layer), *weights[layer], order, blk)
+            todos.append(todo)
+            sent.append(y)
+            return y
+
+        todos = []
         for b in range(batch):
             if done is not None:
-                qkv_all, done = lax.optimization_barrier((qkv_all, done))
-            attn = attention_call(qkv_all, b, 0, 1, seq_len, head_dim, None)
-            groups = [far_first] if b + 1 < batch else [far_first[:tp_size // 2], far_first[tp_size // 2:]]
-            done = None
-            for group in groups:
-                order = jnp.stack([peers[k] for k in group]).astype(jnp.int32)
-                if done is not None:
-                    order, done = lax.optimization_barrier((order, done))
-                    sent[-1] = (sent[-1][0], done, sent[-1][2])
-                done = last_call(residual, attn, *args(layer), *weights[layer], b * seq_len, order, blk)
-                sent.append((b, done, group))
-        for b, y, group in sent:
-            y = y.reshape(len(group), 1, 1, blk, width)
-            for k, piece in zip(group, exchange([(k, y[i]) for i, k in enumerate(group)])):
+                qkv_all, sent[-1] = lax.optimization_barrier((qkv_all, done))
+                done = sent[-1]
+            attn = attention_call(qkv_all, b, b, batch, seq_len, head_dim, attn)
+            done = finish([(b, k) for k in far])
+        finish([(b, k) for b in range(batch) for k in near])
+        y_out = jnp.zeros((tp_size, batch, blk, width), jnp.bfloat16)
+        for todo, y in zip(todos, sent):
+            y = y.reshape(len(todo), 1, 1, blk, width)
+            got = exchange([(k, y[i]) for i, (_, k) in enumerate(todo)])
+            for (b, k), piece in zip(todo, got):
                 y_out = lax.dynamic_update_slice(y_out, piece, (peers[k], b, 0, 0))
         return y_out.reshape(batch_all, blk, width)
 

time: 738 us -> 687 us (0.931)
  Pallas kernels: 509 us -> 490 us
  local copies, waits for them, and re-layouts: 62.6 us -> 46.2 us
  waiting for transfers between devices: 127 us -> 114 us
  blocking collectives: 10.1 us -> 0 us
    ppermute x12 -> x15, waiting for transfers between devices: 114 us -> 92.7 us  [exchange(): lax.ppermute(piece, 'tp', [(i, i ^ k) for i in range(tp_size)])]
    dynamic_update_slice x8 -> x4, local copies, waits for them, and re-layouts: 13.2 us -> 0.04 us  [local_fn(): bup_all = lax.dynamic_update_slice(bup_all, piece[None], (peers[k], 0, 0))]
    slice x6 -> x1, local copies, waits for them, and re-layouts: 12.3 us -> 0.6 us  [args(): return (*norm_args(layer), bsum[layer:layer + 1], bup_all[layer])]
    all_gather x1 -> x0, blocking collectives: 10.1 us -> none  [local_fn(): bup_all = lax.all_gather(half(b_up, 1), ('dp', 'tp'), axis=1, tiled=False)]
    all_gather x8, waiting for transfers between devices: 10.1 us -> 19.6 us  [gather(): return lax.all_gather(shard, ('dp', 'tp'), axis=0, tiled=False)]
    pallas_call x1, Pallas kernels: 137 us -> 128 us  [mid_call(): pl.pallas_call(mid_kernel, grid=(tokens // BLOCK_TOKENS,), in_specs=[row,...]
    pallas_call x4, Pallas kernels: 212 us -> 204 us  [attention_call(): pl.pallas_call(functools.partial(attention_kernel, head_dim=head_dim), gr...]
    dynamic_slice x10 -> x8, local copies, waits for them, and re-layouts: 16.7 us -> 17.3 us  [the longest x6 9.96 us: half(): return lax.dynamic_slice(arr, start, sizes)[0]]
  transfers between devices with their start and end apart: 20 -> 23, of which waited for: 7 -> 5; matrix products, arithmetic and copies ran while one was open for 7% -> 5% of each run, Pallas kernels for 50% -> 56%
where the time goes in v2:
time: 687 us; the launch traced here: 678 us
  Pallas kernels  490 us (71%)
  waiting for transfers between devices  114 us (17%)
  local copies, waits for them, and re-layouts  46.2 us (7%)
  between operations  14 us (2%)
  starting transfers between devices  12.6 us (2%)
    pallas_call x4, Pallas kernels, attention_call(): pl.pallas_call(functools.partial(attention_kernel, head_dim=head_dim), gr...  204 us
    pallas_call x1, Pallas kernels, mid_call(): pl.pallas_call(mid_kernel, grid=(tokens // BLOCK_TOKENS,), in_specs=[row,...  128 us
    pallas_call x3, Pallas kernels, last_call(): pl.pallas_call(last_kernel, grid_spec=pltpu.PrefetchScalarGridSpec(num_sc...  113 us
    ppermute x15, waiting for transfers between devices, exchange(): lax.ppermute(piece, 'tp', [(i, i ^ k) for i in range(tp_size)])  92.7 us
    pallas_call x2, Pallas kernels, qkv_call(): pl.pallas_call(functools.partial(qkv_kernel, pieces=len(received), seq=se...  45.2 us
    all_gather x8, waiting for transfers between devices, gather(): return lax.all_gather(shard, ('dp', 'tp'), axis=0, tiled=False)  19.6 us
  transfers between devices with their start and end apart: 23, of which 5 were waited for; matrix products, arithmetic and copies ran while one was open for 5% of the time, Pallas kernels for 56%

profile of v2, /device:TPU:0, one launch (start us, length us, event | category | flops | bytes accessed | tf_op | source)
XLA Modules:
  0.0 678.3 jit_solution(3549357239571648490)
XLA Ops:
  6.5 1.9 copy-done
  8.4 0.9 constant_dynamic-slice_fusion.4
  9.4 2.3 copy.20
  11.8 0.9 collective-permute-start.3
  12.6 2.5 collective-permute-start.4
  15.1 3.6 constant_dynamic-slice_fusion.9
  18.8 0.1 collective-permute-start
  18.8 1.7 collective-permute-start.1
  20.6 2.3 dynamic-slice_bitcast_fusion
  22.9 2.3 dynamic-slice_bitcast_fusion.1
  25.2 1.7 constant_dynamic-slice_fusion.8
  26.9 0.4 collective-permute-start.5
  27.3 64.8 %collective-permute-done.5 = f32[2,1024]{1,0:T(2,128)S(1)} collective-permute-done((f32[2,1024]{1,0:T(2,128)S(1)}, f32[2,1024]{1,0:T(2,128)S(1)}, u32[]{:S(2)}, u32[]{:S(2)}) %collective-permute-start.5) | collective-permute-done | bytes 8224 | tf_op jit(solution)/shard_map/ppermute | solution.py:372
  92.3 0.1 collective-permute-done.1.refs_1_
  92.4 0.7 all-gather.24.cloned.1.call-update
  93.2 0.5 all-gather.26.cloned.1.call-update
  93.8 0.7 stack.47.place_ref
  94.4 0.6 fusion.3
  95.0 3.7 constant_dynamic-slice_fusion.5
  98.7 1.9 collective-permute-start.7
  100.6 22.6 %ln_qkv.2 = (bf16[4,2048,768]{2,1,0:T(8,128)(2,1)}, bf16[4096,1024]{1,0:T(8,128)(2,1)}) custom-call(s32[5]{0:T(128)} %stack.47.place_ref, bf16[1,1,512,1024]{3,2,1,0:T(8,128)(2,1)} %collective-permute-done.refs_0_, bf16[1,1,512,1024]{3,2,1,0:T(8,128)(2,1)} %collective-permute-done.1.refs_1_, bf16[1,1,512,1024]{3,2,1,0:T(8,128)(2,1)} %collective-permute-done.2.refs_2_, ...), custom_call_target="tpu_custom_call" | custom-call | flops 12884901888 | bytes 23068672 | tf_op jit(solution)/shard_map/ln_qkv/pallas_call | solution.py:106
  123.2 50.8 %causal_attention.4.refs_3_ = bf16[4096,1024]{1,0:T(8,128)(2,1)} custom-call(bf16[4,2048,768]{2,1,0:T(8,128)(2,1)} %get-tuple-element.43.refs_0_.refs_1_.refs_2_, bf16[4,2048,768]{2,1,0:T(8,128)(2,1)} %get-tuple-element.43.refs_0_.refs_1_.refs_2_, bf16[4,2048,768]{2,1,0:T(8,128)(2,1)} %get-tuple-element.43.refs_0_.refs_1_.refs_2_), custom_call_target="tpu_custom_call" | custom-call | flops 28991029248 | bytes 16777216 | tf_op jit(solution)/shard_map/causal_attention/pallas_call | solution.py:200
  174.0 1.0 constant_dynamic-slice_fusion.3
  175.0 2.3 copy.21
  177.4 1.7 constant_dynamic-slice_fusion.2
  179.1 0.5 all-gather.18.cloned.1.call-start
  179.6 2.3 constant_dynamic-slice_fusion.1
  182.1 0.6 pad_add_fusion.1.rows_ref
  182.7 0.6 pad_add_fusion.rows_ref
  183.3 0.7 pad_add_fusion.2.rows_ref
  184.0 0.6 fusion.2
  184.6 0.6 slice_bitcast_fusion.8
  185.2 2.4 constant_dynamic-slice_fusion
  187.6 22.6 %ln_qkv.3 = (bf16[4,2048,768]{2,1,0:T(8,128)(2,1)}, bf16[4096,1024]{1,0:T(8,128)(2,1)}) custom-call(s32[5]{0:T(128)} %stack.47.place_ref, bf16[1,1,512,1024]{3,2,1,0:T(8,128)(2,1)} %collective-permute-done.6.refs_0_, bf16[1,1,512,1024]{3,2,1,0:T(8,128)(2,1)} %collective-permute-done.7.refs_1_, ...), custom_call_target="tpu_custom_call", output_to_operand_aliasing={{1}: (8, {})} | custom-call | flops 12884901888 | bytes 23068672 | tf_op jit(solution)/shard_map/ln_qkv/pallas_call | solution.py:106
  210.2 50.8 %causal_attention.5.o_ref = bf16[4096,1024]{1,0:T(8,128)(2,1)} custom-call(bf16[4,2048,768]{2,1,0:T(8,128)(2,1)} %get-tuple-element.49.refs_0_.refs_1_.refs_2_, bf16[4,2048,768]{2,1,0:T(8,128)(2,1)} %get-tuple-element.49.refs_0_.refs_1_.refs_2_, bf16[4,2048,768]{2,1,0:T(8,128)(2,1)} %get-tuple-element.49.refs_0_.refs_1_.refs_2_, ...), custom_call_target="tpu_custom_call", output_to_operand_aliasing={{}: (3, {})} | custom-call | flops 28991029248 | bytes 16777216 | tf_op jit(solution)/shard_map/causal_attention/pallas_call | solution.py:200
  261.0 19.5 %all-gather.14.cloned.1.call-done.wqkv_hbm = bf16[8,512,768]{2,1,0:T(8,128)(2,1)} async-done(((bf16[1,512,768]{2,1,0:T(8,128)(2,1)}), bf16[8,512,768]{2,1,0:T(8,128)(2,1)}) %all-gather.14.cloned.1.call-update) | async-done | bytes 6291472 | tf_op jit(solution)/shard_map/all_gather | solution.py:355
  280.5 128.4 %ffn_qkv.1 = (f32[4096,1024]{1,0:T(8,128)}, bf16[4,4096,768]{2,1,0:T(8,128)(2,1)}) custom-call(bf16[4096,1024]{1,0:T(8,128)(2,1)} %get-tuple-element.48.r_ref, bf16[4096,1024]{1,0:T(8,128)(2,1)} %causal_attention.5.o_ref, f32[1,1024]{1,0:T(1,128)} %get-tuple-element.87.refs_4_.gain_ref, f32[1,1024]{1,0:T(1,128)} %get-tuple-element.84.refs_5_.bias_ref, ...), custom_call_target="tpu_custom_call" | custom-call | flops 103079215104 | bytes 83886080 | tf_op jit(solution)/shard_map/ffn_qkv/pallas_call | solution.py:297
  408.9 50.9 %causal_attention.6.o_ref.refs_3_ = bf16[4096,1024]{1,0:T(8,128)(2,1)} custom-call(bf16[4,4096,768]{2,1,0:T(8,128)(2,1)} %get-tuple-element.64.refs_0_.refs_1_.refs_2_, bf16[4,4096,768]{2,1,0:T(8,128)(2,1)} %get-tuple-element.64.refs_0_.refs_1_.refs_2_, bf16[4,4096,768]{2,1,0:T(8,128)(2,1)} %get-tuple-element.64.refs_0_.refs_1_.refs_2_), custom_call_target="tpu_custom_call" | custom-call | flops 28991029248 | bytes 16777216 | tf_op jit(solution)/shard_map/causal_attention/pallas_call | solution.py:200
  459.9 29.9 %ffn_out.3 = bf16[1024,1024]{1,0:T(8,128)(2,1)} custom-call(s32[2]{0:T(128)} %pad_add_fusion.1.rows_ref, f32[4096,1024]{1,0:T(8,128)} %get-tuple-element.57.r_ref, bf16[4096,1024]{1,0:T(8,128)(2,1)} %causal_attention.6.o_ref.refs_3_, f32[1,1024]{1,0:T(1,128)} %get-tuple-element.88.ngain_ref.gain_ref, f32[1,1024]{1,0:T(1,128)} %get-tuple-element.83.nbias_ref.bias_ref, ...), custom_call_target="tpu_custom_call" | custom-call | flops 19327352832 | bytes 8388608 | tf_op jit(solution)/shard_map/ffn_out/pallas_call | solution.py:321
  489.7 51.1 %causal_attention.7.o_ref = bf16[4096,1024]{1,0:T(8,128)(2,1)} custom-call(bf16[4,4096,768]{2,1,0:T(8,128)(2,1)} %get-tuple-element.64.refs_0_.refs_1_.refs_2_, bf16[4,4096,768]{2,1,0:T(8,128)(2,1)} %get-tuple-element.64.refs_0_.refs_1_.refs_2_, bf16[4,4096,768]{2,1,0:T(8,128)(2,1)} %get-tuple-element.64.refs_0_.refs_1_.refs_2_, ...), custom_call_target="tpu_custom_call", output_to_operand_aliasing={{}: (3, {})} | custom-call | flops 28991029248 | bytes 16777216 | tf_op jit(solution)/shard_map/causal_attention/pallas_call | solution.py:200
  540.9 30.2 %ffn_out.4 = bf16[1024,1024]{1,0:T(8,128)(2,1)} custom-call(s32[2]{0:T(128)} %pad_add_fusion.rows_ref, f32[4096,1024]{1,0:T(8,128)} %get-tuple-element.57.r_ref, bf16[4096,1024]{1,0:T(8,128)(2,1)} %causal_attention.7.o_ref, f32[1,1024]{1,0:T(1,128)} %get-tuple-element.88.ngain_ref.gain_ref, f32[1,1024]{1,0:T(1,128)} %get-tuple-element.83.nbias_ref.bias_ref, ...), custom_call_target="tpu_custom_call" | custom-call | flops 19327352832 | bytes 8388608 | tf_op jit(solution)/shard_map/ffn_out/pallas_call | solution.py:321
  571.1 3.0 slice_bitcast_fusion.4
  574.1 1.3 collective-permute-start.11
  575.4 1.2 slice_bitcast_fusion.6
  576.6 0.4 collective-permute-start.9
  577.0 1.5 collective-permute-start.10
  578.5 0.6 collective-permute-start.12
  579.0 52.8 %ffn_out.5 = bf16[2048,1024]{1,0:T(8,128)(2,1)} custom-call(s32[4]{0:T(128)} %pad_add_fusion.2.rows_ref, f32[4096,1024]{1,0:T(8,128)} %get-tuple-element.57.r_ref, bf16[4096,1024]{1,0:T(8,128)(2,1)} %causal_attention.7.o_ref, f32[1,1024]{1,0:T(1,128)} %get-tuple-element.88.ngain_ref.gain_ref, f32[1,1024]{1,0:T(1,128)} %get-tuple-element.83.nbias_ref.bias_ref, ...), custom_call_target="tpu_custom_call" | custom-call | flops 38654705664 | bytes 16777216 | tf_op jit(solution)/shard_map/ffn_out/pallas_call | solution.py:321
  631.8 3.1 slice_bitcast_fusion.1
  634.9 1.0 copy-done.5
  635.9 0.5 collective-permute-start.14
  636.4 1.1 broadcast_in_dim.18
  637.5 0.4 copy-done.6
  637.9 0.1 constant_dynamic-update-slice_fusion.5
  638.0 7.3 %collective-permute-done.10 = bf16[1,1,512,1024]{3,2,1,0:T(8,128)(2,1)} collective-permute-done((bf16[1,1,512,1024]{3,2,1,0:T(8,128)(2,1)}, bf16[1,1,512,1024]{3,2,1,0:T(8,128)(2,1)}, u32[]{:S(2)}, u32[]{:S(2)}) %collective-permute-start.10) | collective-permute-done | bytes 1048608 | tf_op jit(solution)/shard_map/ppermute | solution.py:372
  645.2 1.3 constant_dynamic-update-slice_fusion.4
  646.6 0.1 constant_dynamic-update-slice_fusion.3
  646.7 20.5 %collective-permute-done.12 = bf16[1,1,512,1024]{3,2,1,0:T(8,128)(2,1)S(1)} collective-permute-done((bf16[1,1,512,1024]{3,2,1,0:T(8,128)(2,1)}, bf16[1,1,512,1024]{3,2,1,0:T(8,128)(2,1)S(1)}, u32[]{:S(2)}, u32[]{:S(2)}) %collective-permute-start.12) | collective-permute-done | bytes 1048608 | tf_op jit(solution)/shard_map/ppermute | solution.py:372
  667.2 0.1 constant_dynamic-update-slice_fusion.2
  667.3 0.1 constant_dynamic-update-slice_fusion.1
  667.4 0.1 fusion.1
  667.6 0.1 constant_dynamic-update-slice_fusion
  667.7 0.1 fusion
  667.8 3.4 copy-done.2
  (64 shorter events, 0.7 us)
Async XLA Ops:
  6.5 1.9 copy-start
  6.5 18.6 %copy-start.9 = (f32[2,1024]{1,0:T(2,128)S(1)}, f32[2,1024]{1,0:T(2,128)}, u32[]{:S(2)}) copy-start(f32[2,1024]{1,0:T(2,128)} %param.17) | copy-start | bytes 24580
  6.5 94.1 %all-gather.12.cloned.1.call-start = ((), (), s32[]{:S(2)}) async-start(), calls=%async_computation | async-start | bytes 7077888 | tf_op jit(solution)/shard_map/all_gather | solution.py:355
  9.4 85.1 %copy-start.10 = (f32[2,1024]{1,0:T(2,128)S(1)}, f32[2,1024]{1,0:T(2,128)}, u32[]{:S(2)}) copy-start(f32[2,1024]{1,0:T(2,128)} %param.12) | copy-start | bytes 24580
  9.4 85.1 %copy-start.11 = (f32[2,1024]{1,0:T(2,128)S(1)}, f32[2,1024]{1,0:T(2,128)}, u32[]{:S(2)}) copy-start(f32[2,1024]{1,0:T(2,128)} %param.11) | copy-start | bytes 24580
  11.7 249.2 %all-gather.22.cloned.1.call-start = ((), (), s32[]{:S(2)}) async-start(), calls=%async_computation.5 | async-start | bytes 2359296 | tf_op jit(solution)/shard_map/all_gather | solution.py:355
  11.8 15.1 %collective-permute-start.3 = (f32[2,1024]{1,0:T(2,128)}, f32[2,1024]{1,0:T(2,128)S(1)}, u32[]{:S(2)}, u32[]{:S(2)}) collective-permute-start(f32[2,1024]{1,0:T(2,128)} %param.17), channel_id=1, source_target_pairs={{0,1},{1,0},{2,3},{3,2},{4,5},{5,4},{6,7},{7,6}} | collective-permute-start | bytes 24584 | tf_op jit(solution)/shard_map/ppermute | solution.py:372
  12.6 14.7 %collective-permute-start.4 = (f32[2,1024]{1,0:T(2,128)}, f32[2,1024]{1,0:T(2,128)S(1)}, u32[]{:S(2)}, u32[]{:S(2)}) collective-permute-start(f32[2,1024]{1,0:T(2,128)} %param.17), channel_id=1, source_target_pairs={{0,2},{1,3},{2,0},{3,1},{4,6},{5,7},{6,4},{7,5}} | collective-permute-start | bytes 24584 | tf_op jit(solution)/shard_map/ppermute | solution.py:372
  18.8 73.5 %collective-permute-start = (bf16[1,1,512,1024]{3,2,1,0:T(8,128)(2,1)}, bf16[1,1,512,1024]{3,2,1,0:T(8,128)(2,1)}, u32[]{:S(2)}, u32[]{:S(2)}) collective-permute-start(bf16[1,1,512,1024]{3,2,1,0:T(8,128)(2,1)} %get-tuple-element.72), channel_id=1, source_target_pairs={{0,3},{1,2},{2,1},{3,0},{4,7},{5,6},{6,5},{7,4}} | collective-permute-start | bytes 3145736 | tf_op jit(solution)/shard_map/ppermute | solution.py:372
  18.8 73.5 %collective-permute-start.1 = (bf16[1,1,512,1024]{3,2,1,0:T(8,128)(2,1)}, bf16[1,1,512,1024]{3,2,1,0:T(8,128)(2,1)}, u32[]{:S(2)}, u32[]{:S(2)}) collective-permute-start(bf16[1,1,512,1024]{3,2,1,0:T(8,128)(2,1)} %get-tuple-element.71), channel_id=1, source_target_pairs={{0,2},{1,3},{2,0},{3,1},{4,6},{5,7},{6,4},{7,5}} | collective-permute-start | bytes 3145736 | tf_op jit(solution)/shard_map/ppermute | solution.py:372
  20.6 71.8 %collective-permute-start.2 = (bf16[1,1,512,1024]{3,2,1,0:T(8,128)(2,1)}, bf16[1,1,512,1024]{3,2,1,0:T(8,128)(2,1)}, u32[]{:S(2)}, u32[]{:S(2)}) collective-permute-start(bf16[1,1,512,1024]{3,2,1,0:T(8,128)(2,1)} %get-tuple-element.70), channel_id=1, source_target_pairs={{0,1},{1,0},{2,3},{3,2},{4,5},{5,4},{6,7},{7,6}} | collective-permute-start | bytes 3145736 | tf_op jit(solution)/shard_map/ppermute | solution.py:372
  26.9 65.2 %collective-permute-start.5 = (f32[2,1024]{1,0:T(2,128)S(1)}, f32[2,1024]{1,0:T(2,128)S(1)}, u32[]{:S(2)}, u32[]{:S(2)}) collective-permute-start(f32[2,1024]{1,0:T(2,128)S(1)} %copy-done.9), channel_id=1, source_target_pairs={{0,3},{1,2},{2,1},{3,0},{4,7},{5,6},{6,5},{7,4}} | collective-permute-start | bytes 24584 | tf_op jit(solution)/shard_map/ppermute | solution.py:372
  92.4 168.6 %all-gather.24.cloned.1.call-start = ((), (), s32[]{:S(2)}) async-start(), calls=%async_computation.6 | async-start | bytes 9437184 | tf_op jit(solution)/shard_map/all_gather | solution.py:355
  93.1 167.8 %all-gather.26.cloned.1.call-start = ((), (), s32[]{:S(2)}) async-start(), calls=%async_computation.7 | async-start | bytes 9437184 | tf_op jit(solution)/shard_map/all_gather | solution.py:355
  93.7 186.8 %all-gather.14.cloned.1.call-start = ((), (), s32[]{:S(2)}) async-start(), calls=%async_computation.1 | async-start | bytes 7077888 | tf_op jit(solution)/shard_map/all_gather | solution.py:355
  98.7 75.3 %collective-permute-start.6 = (bf16[1,1,512,1024]{3,2,1,0:T(8,128)(2,1)}, bf16[1,1,512,1024]{3,2,1,0:T(8,128)(2,1)}, u32[]{:S(2)}, u32[]{:S(2)}) collective-permute-start(bf16[1,1,512,1024]{3,2,1,0:T(8,128)(2,1)} %get-tuple-element.69), channel_id=1, source_target_pairs={{0,3},{1,2},{2,1},{3,0},{4,7},{5,6},{6,5},{7,4}} | collective-permute-start | bytes 3145736 | tf_op jit(solution)/shard_map/ppermute | solution.py:372
  98.7 75.3 %collective-permute-start.7 = (bf16[1,1,512,1024]{3,2,1,0:T(8,128)(2,1)}, bf16[1,1,512,1024]{3,2,1,0:T(8,128)(2,1)}, u32[]{:S(2)}, u32[]{:S(2)}) collective-permute-start(bf16[1,1,512,1024]{3,2,1,0:T(8,128)(2,1)} %get-tuple-element.68), channel_id=1, source_target_pairs={{0,2},{1,3},{2,0},{3,1},{4,6},{5,7},{6,4},{7,5}} | collective-permute-start | bytes 3145736 | tf_op jit(solution)/shard_map/ppermute | solution.py:372
  100.6 73.4 %collective-permute-start.8 = (bf16[1,1,512,1024]{3,2,1,0:T(8,128)(2,1)}, bf16[1,1,512,1024]{3,2,1,0:T(8,128)(2,1)}, u32[]{:S(2)}, u32[]{:S(2)}) collective-permute-start(bf16[1,1,512,1024]{3,2,1,0:T(8,128)(2,1)} %get-tuple-element.67), channel_id=1, source_target_pairs={{0,1},{1,0},{2,3},{3,2},{4,5},{5,4},{6,7},{7,6}} | collective-permute-start | bytes 3145736 | tf_op jit(solution)/shard_map/ppermute | solution.py:372
  123.2 58.8 %copy-start.7 = (f32[2,1024]{1,0:T(2,128)S(1)}, f32[2,1024]{1,0:T(2,128)}, u32[]{:S(2)}) copy-start(f32[2,1024]{1,0:T(2,128)} %param.15) | copy-start | bytes 24580
  123.2 58.8 %copy-start.8 = (f32[2,1024]{1,0:T(2,128)S(1)}, f32[2,1024]{1,0:T(2,128)}, u32[]{:S(2)}) copy-start(f32[2,1024]{1,0:T(2,128)} %param.19) | copy-start | bytes 24580
  177.4 282.5 %all-gather.16.cloned.1.call-start = ((), (), s32[]{:S(2)}) async-start(), calls=%async_computation.2 | async-start | bytes 2359296 | tf_op jit(solution)/shard_map/all_gather | solution.py:355
  179.1 280.7 %all-gather.18.cloned.1.call-start = ((), (), s32[]{:S(2)}) async-start(), calls=%async_computation.3 | async-start | bytes 9437184 | tf_op jit(solution)/shard_map/all_gather | solution.py:355
  182.0 277.9 %all-gather.20.cloned.1.call-start = ((), (), s32[]{:S(2)}) async-start(), calls=%async_computation.4 | async-start | bytes 9437184 | tf_op jit(solution)/shard_map/all_gather | solution.py:355
  540.9 34.5 %copy-start.4 = (bf16[1024,1024]{1,0:T(8,128)(2,1)S(1)}, bf16[1024,1024]{1,0:T(8,128)(2,1)}, u32[]{:S(2)}) copy-start(bf16[1024,1024]{1,0:T(8,128)(2,1)} %ffn_out.3) | copy-start | bytes 6291460
  574.1 72.5 %collective-permute-start.11 = (bf16[1,1,512,1024]{3,2,1,0:T(8,128)(2,1)}, bf16[1,1,512,1024]{3,2,1,0:T(8,128)(2,1)S(1)}, u32[]{:S(2)}, u32[]{:S(2)}) collective-permute-start(bf16[1,1,512,1024]{3,2,1,0:T(8,128)(2,1)} %get-tuple-element.76), channel_id=1, source_target_pairs={{0,3},{1,2},{2,1},{3,0},{4,7},{5,6},{6,5},{7,4}} | collective-permute-start | bytes 3145736 | tf_op jit(solution)/shard_map/ppermute | solution.py:372
  576.6 58.3 %collective-permute-start.9 = (bf16[1,1,512,1024]{3,2,1,0:T(8,128)(2,1)S(1)}, bf16[1,1,512,1024]{3,2,1,0:T(8,128)(2,1)S(1)}, u32[]{:S(2)}, u32[]{:S(2)}) collective-permute-start(bf16[1,1,512,1024]{3,2,1,0:T(8,128)(2,1)S(1)} %get-tuple-element.78), channel_id=1, source_target_pairs={{0,3},{1,2},{2,1},{3,0},{4,7},{5,6},{6,5},{7,4}} | collective-permute-start | bytes 3145736 | tf_op jit(solution)/shard_map/ppermute | solution.py:372
  577.0 68.2 %collective-permute-start.10 = (bf16[1,1,512,1024]{3,2,1,0:T(8,128)(2,1)}, bf16[1,1,512,1024]{3,2,1,0:T(8,128)(2,1)}, u32[]{:S(2)}, u32[]{:S(2)}) collective-permute-start(bf16[1,1,512,1024]{3,2,1,0:T(8,128)(2,1)} %get-tuple-element.77), channel_id=1, source_target_pairs={{0,2},{1,3},{2,0},{3,1},{4,6},{5,7},{6,4},{7,5}} | collective-permute-start | bytes 3145736 | tf_op jit(solution)/shard_map/ppermute | solution.py:372
  578.5 88.7 %collective-permute-start.12 = (bf16[1,1,512,1024]{3,2,1,0:T(8,128)(2,1)}, bf16[1,1,512,1024]{3,2,1,0:T(8,128)(2,1)S(1)}, u32[]{:S(2)}, u32[]{:S(2)}) collective-permute-start(bf16[1,1,512,1024]{3,2,1,0:T(8,128)(2,1)} %get-tuple-element.75), channel_id=1, source_target_pairs={{0,2},{1,3},{2,0},{3,1},{4,6},{5,7},{6,4},{7,5}} | collective-permute-start | bytes 3145736 | tf_op jit(solution)/shard_map/ppermute | solution.py:372
  634.9 32.4 %collective-permute-start.13 = (bf16[1,1,512,1024]{3,2,1,0:T(8,128)(2,1)}, bf16[1,1,512,1024]{3,2,1,0:T(8,128)(2,1)S(1)}, u32[]{:S(2)}, u32[]{:S(2)}) collective-permute-start(bf16[1,1,512,1024]{3,2,1,0:T(8,128)(2,1)} %get-tuple-element.74), channel_id=1, source_target_pairs={{0,1},{1,0},{2,3},{3,2},{4,5},{5,4},{6,7},{7,6}} | collective-permute-start | bytes 3145736 | tf_op jit(solution)/shard_map/ppermute | solution.py:372
  634.9 1.0 copy-start.5
  635.9 31.6 %copy-start.3 = (bf16[2048,1024]{1,0:T(8,128)(2,1)S(1)}, bf16[2048,1024]{1,0:T(8,128)(2,1)}, u32[]{:S(2)}) copy-start(bf16[2048,1024]{1,0:T(8,128)(2,1)} %ffn_out.5) | copy-start | bytes 12582916
  635.9 31.7 %collective-permute-start.14 = (bf16[1,1,512,1024]{3,2,1,0:T(8,128)(2,1)}, bf16[1,1,512,1024]{3,2,1,0:T(8,128)(2,1)S(1)}, u32[]{:S(2)}, u32[]{:S(2)}) collective-permute-start(bf16[1,1,512,1024]{3,2,1,0:T(8,128)(2,1)} %get-tuple-element.73), channel_id=1, source_target_pairs={{0,1},{1,0},{2,3},{3,2},{4,5},{5,4},{6,7},{7,6}} | collective-permute-start | bytes 3145736 | tf_op jit(solution)/shard_map/ppermute | solution.py:372
  636.4 1.5 copy-start.6
  636.4 34.8 %copy-start.1 = (bf16[2,1024,3,4,64]{1,4,3,2,0:T(8,128)(2,1)S(1)}, bf16[2,1024,3,4,64]{1,4,3,2,0:T(8,128)(2,1)}, u32[]{:S(2)}) copy-start(bf16[2,1024,3,4,64]{1,4,3,2,0:T(8,128)(2,1)} %param.13) | copy-start | bytes 9437188
  667.8 3.4 copy-start.2
Sparse Core Ops, SparseCore 0:
  11.8 67.4 all-gather.11
  92.5 28.7 all-gather.21
  123.2 65.3 all-gather.23
  190.3 48.6 all-gather.25
  240.7 39.8 all-gather.13
  282.2 22.2 all-gather.15
  306.3 48.6 all-gather.17
  356.8 48.6 all-gather.19

commit v3 on v2

--- a/solution.py
+++ b/solution.py
@@ -5,6 +5,7 @@
 import jax.numpy as jnp
 from jax import lax
 from jax.experimental import pallas as pl
+from jax.experimental.layout import Layout, with_layout_constraint
 from jax.experimental.pallas import tpu as pltpu
 from jax.sharding import PartitionSpec as P
 
@@ -56,15 +57,37 @@
         pltpu.make_async_copy(w_hbm.at[i], w_vmem.at[chunk, pl.ds(half * rows, rows)], sem).wait()
 
 
-def project_qkv(h, w_vmem, qkv_ref, rows):
+def project_qkv(h, w_vmem, qkv_ref):
     for c in range(w_vmem.shape[0]):
-        qkv_ref[c, rows, :] = dot(h, w_vmem[c]).astype(jnp.bfloat16)
-
-
-def norm_project(x_of, splits, gain_ref, bias_ref, w_vmem, qkv_ref):
-    for lo, hi in splits:
-        h = layer_norm(x_of(lo, hi), gain_ref[...], bias_ref[...])
-        project_qkv(h, w_vmem, qkv_ref, slice(lo, hi))
+        qkv_ref[c] = dot(h, w_vmem[c]).astype(jnp.bfloat16)
+
+
+def next_qkv_kernel(r_ref, gain_ref, bias_ref, w_hbm, qkv_ref, w_vmem, sem):
+    @pl.when(pl.program_id(0) == 0)
+    def _():
+        start_qkv_copies(w_hbm, w_vmem, sem)
+        wait_qkv_copies(w_hbm, w_vmem, sem)
+
+    project_qkv(layer_norm(r_ref[...], gain_ref[...], bias_ref[...]), w_vmem, qkv_ref)
+
+
+def next_qkv_call(r, gain, bias, w_qkv):
+    tokens, width = r.shape
+    parts, rows, cols = w_qkv.shape
+    chunks = parts * rows // width
+    vec = pl.BlockSpec((1, width), lambda i: (0, 0))
+    return pl.pallas_call(
+        next_qkv_kernel,
+        grid=(tokens // BLOCK_TOKENS,),
+        in_specs=[pl.BlockSpec((BLOCK_TOKENS, width), lambda i: (i, 0)), vec, vec, pl.BlockSpec(memory_space=pl.ANY)],
+        out_specs=pl.BlockSpec((chunks, BLOCK_TOKENS, cols), lambda i: (0, i, 0)),
+        out_shape=jax.ShapeDtypeStruct((chunks, tokens, cols), jnp.bfloat16),
+        scratch_shapes=[pltpu.VMEM((chunks, width, cols), jnp.bfloat16), pltpu.SemaphoreType.DMA],
+        compiler_params=pltpu.CompilerParams(
+            dimension_semantics=('arbitrary',), vmem_limit_bytes=VMEM_LIMIT),
+        cost_estimate=cost(2 * tokens * width * chunks * cols, 2 * tokens * (2 * width + chunks * cols)),
+        name='next_qkv',
+    )(r, gain, bias, w_qkv)
 
 
 def qkv_kernel(place_ref, *refs, pieces, seq):
@@ -88,9 +111,8 @@
 
     row0 = pl.multiple_of(step * BLOCK_TOKENS, BLOCK_TOKENS)
     res_ref[...] = x_vmem[pl.ds(row0, BLOCK_TOKENS), :]
-    quarter = BLOCK_TOKENS // 4
-    norm_project(lambda lo, hi: x_vmem[pl.ds(row0 + lo, hi - lo), :].astype(jnp.float32),
-                 ((0, quarter), (quarter, BLOCK_TOKENS)), gain_ref, bias_ref, w_vmem, qkv_ref)
+    h = layer_norm(x_vmem[pl.ds(row0, BLOCK_TOKENS), :].astype(jnp.float32), gain_ref[...], bias_ref[...])
+    project_qkv(h, w_vmem, qkv_ref)
 
 
 def qkv_call(place, received, x_own, seq, batch, gain, bias, w_qkv, buffer):
@@ -134,61 +156,53 @@
         vx_ref[:, pair:] = jnp.ones((seq_len, pair), jnp.bfloat16)
 
     low_lane = lax.broadcasted_iota(jnp.int32, (1, pair), 1) < head_dim
-    q_pos = lax.broadcasted_iota(jnp.int32, (BLOCK_Q, BLOCK_K), 0)
-    k_pos = lax.broadcasted_iota(jnp.int32, (BLOCK_Q, BLOCK_K), 1)
+    rows = 2 * BLOCK_Q
+    q_pos = lax.broadcasted_iota(jnp.int32, (rows, BLOCK_K), 0) % BLOCK_Q
+    k_pos = lax.broadcasted_iota(jnp.int32, (rows, BLOCK_K), 1)
     causal = k_pos <= q_pos
     inv_sqrt = head_dim ** -0.5
     n_blocks = seq_len // BLOCK_Q
-    order = list(range(0, n_blocks, 2)) + list(range(1, n_blocks, 2))[::-1]
-    units = [(block, head) for block in order for head in range(2)]
-
-    def head_query(unit):
-        block, head = unit
+    units = list(range(0, n_blocks, 2)) + list(range(1, n_blocks, 2))[::-1]
+
+    def stacked_query(block):
         q_blk = q_ref[0, block * BLOCK_Q:(block + 1) * BLOCK_Q, :] * jnp.bfloat16(inv_sqrt)
-        keep = low_lane if head == 0 else jnp.logical_not(low_lane)
-        return jnp.where(keep, q_blk, jnp.zeros_like(q_blk))
-
-    def score_chunk(unit_idx, q_h, c, run_max):
-        block, _ = units[unit_idx]
+        zero = jnp.zeros_like(q_blk)
+        return jnp.concatenate([jnp.where(low_lane, q_blk, zero), jnp.where(low_lane, zero, q_blk)], axis=0)
+
+    def score_chunk(slot, block, q_h, c, run_max):
         k_blk = k_ref[0, c * BLOCK_K:(c + 1) * BLOCK_K, :]
         s = lax.dot_general(q_h, k_blk, (((1,), (1,)), ((), ())), preferred_element_type=jnp.float32)
         if c == block:
             s = jnp.where(causal, s, -jnp.inf)
-        s_ref[unit_idx % 2, :, c * BLOCK_K:(c + 1) * BLOCK_K] = s
+        s_ref[slot, :, c * BLOCK_K:(c + 1) * BLOCK_K] = s
         chunk_max = s[:, :128]
         for j in range(1, BLOCK_K // 128):
             chunk_max = jnp.maximum(chunk_max, s[:, j * 128:(j + 1) * 128])
         return chunk_max if run_max is None else jnp.maximum(run_max, chunk_max)
 
-    def value_chunk(unit_idx, row_max, c):
-        s = s_ref[unit_idx % 2, :, c * BLOCK_K:(c + 1) * BLOCK_K]
+    def value_chunk(slot, row_max, c):
+        s = s_ref[slot, :, c * BLOCK_K:(c + 1) * BLOCK_K]
         p = jnp.exp2((s - row_max) * LOG2_E).astype(jnp.bfloat16)
         return dot(p, vx_ref[c * BLOCK_K:(c + 1) * BLOCK_K, :])
 
     run_max = None
-    row_max = None
-    held = None
     for step in range(len(units) + 1):
-        n_score = units[step][0] + 1 if step < len(units) else 0
-        n_value = units[step - 1][0] + 1 if step > 0 else 0
-        if step > 0:
-            row_max = jnp.max(run_max, axis=1, keepdims=True)
+        n_score = units[step] + 1 if step < len(units) else 0
+        n_value = units[step - 1] + 1 if step > 0 else 0
+        row_max = jnp.max(run_max, axis=1, keepdims=True) if step > 0 else None
         run_max = None
         acc = None
-        q_h = head_query(units[step]) if n_score else None
+        q_h = stacked_query(units[step]) if n_score else None
         for c in range(max(n_score, n_value)):
             if c < n_score:
-                run_max = score_chunk(step, q_h, c, run_max)
+                run_max = score_chunk(step % 2, units[step], q_h, c, run_max)
             if c < n_value:
-                part = value_chunk(step - 1, row_max, c)
+                part = value_chunk((step - 1) % 2, row_max, c)
                 acc = part if acc is None else acc + part
         if n_value:
-            block, head = units[step - 1]
+            block = units[step - 1]
             out = acc[:, :pair] / acc[:, pair:]
-            if head == 0:
-                held = out
-            else:
-                o_ref[block * BLOCK_Q:(block + 1) * BLOCK_Q, :] = jnp.where(low_lane, held, out).astype(jnp.bfloat16)
+            o_ref[block * BLOCK_Q:(block + 1) * BLOCK_Q, :] = jnp.where(low_lane, out[:BLOCK_Q], out[BLOCK_Q:]).astype(jnp.bfloat16)
 
 
 def attention_call(qkv, qkv_seq, seq, batch, seq_len, head_dim, buffer):
@@ -204,7 +218,7 @@
         out_specs=pl.BlockSpec((seq_len, pair), lambda g: (seq, g)),
         out_shape=jax.ShapeDtypeStruct((batch * seq_len, chunks * subs * pair), jnp.bfloat16),
         input_output_aliases={3: 0} if held else {},
-        scratch_shapes=[pltpu.VMEM((2, BLOCK_Q, seq_len), jnp.float32), pltpu.VMEM((seq_len, 2 * pair), jnp.bfloat16)],
+        scratch_shapes=[pltpu.VMEM((2, 2 * BLOCK_Q, seq_len), jnp.float32), pltpu.VMEM((seq_len, 2 * pair), jnp.bfloat16)],
         compiler_params=pltpu.CompilerParams(
             dimension_semantics=('arbitrary',), vmem_limit_bytes=VMEM_LIMIT),
         cost_estimate=cost(9 * seq_len * seq_len * chunks * cols // 4, 2 * seq_len * chunks * (cols + subs * pair)),
@@ -213,7 +227,7 @@
 
 
 def ffn_body(first, r_ref, o_ref, gain_ref, bias_ref, bsum_ref, bup_ref, wout_hbm, wup_hbm, wdown_hbm,
-             acc_ref, wout_vmem, wup_vmem, wdown_vmem, sems, emit, more_waits=lambda: None):
+             acc_ref, wout_vmem, wup_vmem, wdown_vmem, sems, emit):
     parts = wup_vmem.shape[0]
     early = 2
     out_rows = wout_hbm.shape[1]
@@ -243,7 +257,6 @@
             def _():
                 for cp in late_copies:
                     cp.wait()
-                more_waits()
         ahead = dot(h, wup_vmem[c + 1]) + bup_ref[c + 1] if c + 1 < parts else None
         gelu_out = gelu_tanh(hidden).astype(jnp.bfloat16)
         if c + 1 < parts:
@@ -254,64 +267,18 @@
         hidden = ahead
 
 
-def mid_kernel(r_ref, o_ref, gain_ref, bias_ref, bsum_ref, bup_ref, ngain_ref, nbias_ref, wout_hbm, wup_hbm, wdown_hbm,
-               wqkv_hbm, res_ref, qkv_ref, acc_ref, wout_vmem, wup_vmem, wdown_vmem, wqkv_vmem, sems):
-    first = pl.program_id(0) == 0
-
-    @pl.when(first)
-    def _():
-        start_qkv_copies(wqkv_hbm, wqkv_vmem, sems.at[2])
-
-    rows_done = []
-
-    def emit(rows, r_new):
-        res_ref[rows, :] = r_new
-        rows_done.append((rows, r_new))
-
-    ffn_body(first, r_ref, o_ref, gain_ref, bias_ref, bsum_ref, bup_ref, wout_hbm, wup_hbm, wdown_hbm,
-             acc_ref, wout_vmem, wup_vmem, wdown_vmem, sems, emit,
-             lambda: wait_qkv_copies(wqkv_hbm, wqkv_vmem, sems.at[2]))
-    for rows, r_new in rows_done:
-        project_qkv(layer_norm(r_new, ngain_ref[...], nbias_ref[...]), wqkv_vmem, qkv_ref, rows)
-
-
-def last_kernel(rows_ref, r_ref, o_ref, gain_ref, bias_ref, bsum_ref, bup_ref, wout_hbm, wup_hbm, wdown_hbm,
+def block_kernel(rows_ref, r_ref, o_ref, gain_ref, bias_ref, bsum_ref, bup_ref, wout_hbm, wup_hbm, wdown_hbm,
                 y_ref, acc_ref, wout_vmem, wup_vmem, wdown_vmem, sems):
     first = pl.program_id(0) == 0
 
     def emit(rows, r_new):
-        y_ref[rows, :] = r_new.astype(jnp.bfloat16)
+        y_ref[rows, :] = r_new.astype(y_ref.dtype)
 
     ffn_body(first, r_ref, o_ref, gain_ref, bias_ref, bsum_ref, bup_ref, wout_hbm, wup_hbm, wdown_hbm,
              acc_ref, wout_vmem, wup_vmem, wdown_vmem, sems, emit)
 
 
-def mid_call(r, o, gain, bias, bsum, bup, ngain, nbias, w_out, w_up, w_down, w_qkv):
-    tokens, width = r.shape
-    parts, rows, cols = w_qkv.shape
-    chunks = parts * rows // width
-    row = pl.BlockSpec((BLOCK_TOKENS, width), lambda i: (i, 0))
-    vec = pl.BlockSpec((1, width), lambda i: (0, 0))
-    bup_spec = pl.BlockSpec(bup.shape, lambda i: (0, 0, 0))
-    hbm = pl.BlockSpec(memory_space=pl.ANY)
-    return pl.pallas_call(
-        mid_kernel,
-        grid=(tokens // BLOCK_TOKENS,),
-        in_specs=[row, row, vec, vec, vec, bup_spec, vec, vec, hbm, hbm, hbm, hbm],
-        out_specs=[row, pl.BlockSpec((chunks, BLOCK_TOKENS, cols), lambda i: (0, i, 0))],
-        out_shape=[jax.ShapeDtypeStruct((tokens, width), jnp.float32),
-                   jax.ShapeDtypeStruct((chunks, tokens, cols), jnp.bfloat16)],
-        scratch_shapes=[pltpu.VMEM((BLOCK_TOKENS, width), jnp.float32), pltpu.VMEM((width, width), jnp.bfloat16),
-                        pltpu.VMEM(w_up.shape, jnp.bfloat16), pltpu.VMEM(w_down.shape, jnp.bfloat16),
-                        pltpu.VMEM((chunks, width, cols), jnp.bfloat16), pltpu.SemaphoreType.DMA((3,))],
-        compiler_params=pltpu.CompilerParams(
-            dimension_semantics=('arbitrary',), vmem_limit_bytes=VMEM_LIMIT),
-        cost_estimate=cost(24 * tokens * width * width, 20 * tokens * width),
-        name='ffn_qkv',
-    )(r, o, gain, bias, bsum, bup, ngain, nbias, w_out, w_up, w_down, w_qkv)
-
-
-def last_call(r, o, gain, bias, bsum, bup, w_out, w_up, w_down, blocks, blk):
+def block_call(r, o, gain, bias, bsum, bup, w_out, w_up, w_down, blocks, blk, dtype):
     width = r.shape[1]
     count = blocks.shape[0] * blk
     per = blk // BLOCK_TOKENS
@@ -319,7 +286,7 @@
     vec = pl.BlockSpec((1, width), lambda i, rows: (0, 0))
     hbm = pl.BlockSpec(memory_space=pl.ANY)
     return pl.pallas_call(
-        last_kernel,
+        block_kernel,
         grid_spec=pltpu.PrefetchScalarGridSpec(
             num_scalar_prefetch=1,
             grid=(count // BLOCK_TOKENS,),
@@ -329,11 +296,11 @@
             scratch_shapes=[pltpu.VMEM((BLOCK_TOKENS, width), jnp.float32), pltpu.VMEM((width, width), jnp.bfloat16),
                             pltpu.VMEM(w_up.shape, jnp.bfloat16), pltpu.VMEM(w_down.shape, jnp.bfloat16),
                             pltpu.SemaphoreType.DMA((2,))]),
-        out_shape=jax.ShapeDtypeStruct((count, width), jnp.bfloat16),
+        out_shape=jax.ShapeDtypeStruct((count, width), dtype),
         compiler_params=pltpu.CompilerParams(
             dimension_semantics=('arbitrary',), vmem_limit_bytes=VMEM_LIMIT),
         cost_estimate=cost(18 * count * width * width, 8 * count * width),
-        name='ffn_out',
+        name='ffn',
     )(blocks, r, o, gain, bias, bsum, bup, w_out, w_up, w_down)
 
 
@@ -382,70 +349,74 @@
         x_parts = x_in.reshape(tp_size, batch, blk, width)
         place = jnp.stack([peers[k] for k in far_first] + [jnp.full_like(tp_idx, batch)]).astype(jnp.int32)
 
-        def x_send(parts, b):
-            return [(k, lax.dynamic_slice(parts, (peers[k], b, 0, 0), (1, 1, blk, width))) for k in far_first if k]
-
+        links = [k for k in far_first if k]
         first_shard = qkv_shard(0, w_qkv)
+        later_parts, _ = lax.optimization_barrier((x_parts, first_shard))
+        x_send = [[lax.dynamic_slice(later_parts if b else x_parts, (peers[k], b, 0, 0), (1, 1, blk, width)) for k in links]
+                  for b in range(batch)]
         qkv_w = gather(first_shard)
-        received = exchange(x_send(x_parts, 0))
+        received = exchange(zip(links, x_send[0]))
         biases = exchange([(k, b_up) for k in range(tp_size)])
         bup_all = jnp.zeros((tp_size, n_layers, ffn), jnp.float32)
         for k, piece in enumerate(biases):
             bup_all = lax.dynamic_update_slice(bup_all, piece[None], (peers[k], 0, 0))
         bup_all = bup_all.reshape(tp_size, n_layers, dp_size, ffn // dp_size).transpose(1, 2, 0, 3)
         bup_all = bup_all.reshape(n_layers, dp_size * tp_size, 1, ffn // dp_size)
-        first_shard, received, bup_all = lax.optimization_barrier((first_shard, received, bup_all))
-        received, x_later, shards = lax.optimization_barrier((received, x_parts, ffn_shards(0, w_out, w_up, w_down)))
-        pieces = [received] + [exchange(x_send(x_later, b)) for b in range(1, batch)]
-        weights = [ffn_weights(shards)]
+        small = [(ln_gain[layer:layer + 1], ln_bias[layer:layer + 1], bsum[layer:layer + 1], bup_all[layer])
+                 for layer in range(n_layers)]
+
+        far, near = far_first[:tp_size // 2], far_first[tp_size // 2:]
+        todos = [[(b, k) for k in far] for b in range(batch)] + [[(b, k) for b in range(batch) for k in near]]
+        orders = [jnp.stack([b * tp_size + peers[k] for b, k in todo]).astype(jnp.int32) for todo in todos]
+
+        shards = [ffn_shards(layer, w_out, w_up, w_down) for layer in range(n_layers)]
+        qkv_shards = [with_layout_constraint(qkv_shard(layer, w_qkv), Layout(major_to_minor=(0, 1)))
+                      for layer in range(1, n_layers)]
+        received, small, orders, place, shards, qkv_shards, x_send[1:] = lax.optimization_barrier(
+            (received, small, orders, place, shards, qkv_shards, x_send[1:]))
+        pieces = [received] + [exchange(zip(links, x_send[b])) for b in range(1, batch)]
+        weights = [ffn_weights(shards[0])]
 
         def norm_args(layer):
-            return ln_gain[layer:layer + 1], ln_bias[layer:layer + 1]
+            return small[layer][:2]
 
         qkv, residual, attn = None, None, None
-        params = (w_qkv, w_out, w_up, w_down)
         for b in range(batch):
             got = pieces[b]
             if b:
-                got, attn, params = lax.optimization_barrier((got, attn, params))
+                got, attn, shards, qkv_shards = lax.optimization_barrier((got, attn, shards, qkv_shards))
             qkv, residual = qkv_call(place, got, x_in, b, batch, *norm_args(0), qkv_w, residual)
             attn = attention_call(qkv, 0, b, batch, seq_len, head_dim, attn)
         later_qkv = []
         for layer in range(1, n_layers):
-            later_qkv.append(gather(qkv_shard(layer, params[0])))
-            weights.append(ffn_weights(ffn_shards(layer, *params[1:])))
-
-        def args(layer):
-            return (*norm_args(layer), bsum[layer:layer + 1], bup_all[layer])
+            later_qkv.append(gather(qkv_shards[layer - 1]))
+            weights.append(ffn_weights(shards[layer]))
 
         for layer in range(n_layers - 1):
             if layer:
                 attn = None
                 for b in range(batch):
                     attn = attention_call(qkv_all, b, b, batch, seq_len, head_dim, attn)
-            residual, qkv_all = mid_call(residual, attn, *args(layer), *norm_args(layer + 1), *weights[layer],
-                                         later_qkv[layer])
+            everything = jnp.arange(batch * tp_size, dtype=jnp.int32)
+            residual = block_call(residual, attn, *small[layer], *weights[layer], everything, blk, jnp.float32)
+            qkv_all = next_qkv_call(residual, *norm_args(layer + 1), later_qkv[layer])
         layer = n_layers - 1
-        far, near = far_first[:tp_size // 2], far_first[tp_size // 2:]
         attn, done, sent = None, None, []
 
-        def finish(todo):
-            order = jnp.stack([b * tp_size + peers[k] for b, k in todo]).astype(jnp.int32)
+        def finish(order):
             if done is not None:
                 order, sent[-1] = lax.optimization_barrier((order, done))
-            y = last_call(residual, attn, *args(layer), *weights[layer], order, blk)
-            todos.append(todo)
+            y = block_call(residual, attn, *small[layer], *weights[layer], order, blk, jnp.bfloat16)
             sent.append(y)
             return y
 
-        todos = []
         for b in range(batch):
             if done is not None:
                 qkv_all, sent[-1] = lax.optimization_barrier((qkv_all, done))
                 done = sent[-1]
             attn = attention_call(qkv_all, b, b, batch, seq_len, head_dim, attn)
-            done = finish([(b, k) for k in far])
-        finish([(b, k) for b in range(batch) for k in near])
+            done = finish(orders[b])
+        finish(orders[batch])
         y_out = jnp.zeros((tp_size, batch, blk, width), jnp.bfloat16)
         for todo, y in zip(todos, sent):
             y = y.reshape(len(todo), 1, 1, blk, width)

time: 687 us -> 678 us (0.987)
  local copies, waits for them, and re-layouts: 46.2 us -> 32.4 us
  waiting for transfers between devices: 114 us -> 121 us
    ppermute x15, waiting for transfers between devices: 92.7 us -> 118 us  [exchange(): lax.ppermute(piece, 'tp', [(i, i ^ k) for i in range(tp_size)])]
    all_gather x8, waiting for transfers between devices: 19.6 us -> 0.05 us  [gather(): return lax.all_gather(shard, ('dp', 'tp'), axis=0, tiled=False)]
    pallas_call x4, Pallas kernels: 204 us -> 193 us  [attention_call(): pl.pallas_call(functools.partial(attention_kernel, head_dim=head_dim), gr...]
    pallas_call x4 -> x5, Pallas kernels: 241 us -> 249 us  [the longest x4 212 us: block_call(): pl.pallas_call(block_kernel, grid_spec=pltpu.PrefetchScalarGridSpec(num_s...]
    dynamic_slice x6 -> x2, local copies, waits for them, and re-layouts: 9.96 us -> 2.45 us  [half(): return lax.dynamic_slice(arr, start, sizes)[0]]
  transfers between devices with their start and end apart: 23 -> 23, of which waited for: 5 -> 4; matrix products, arithmetic and copies ran while one was open for 5% -> 4% of each run, Pallas kernels for 56% -> 57%
where the time goes in v3:
time: 678 us; the launch traced here: 669 us
  Pallas kernels  489 us (72%)
  waiting for transfers between devices  121 us (18%)
  local copies, waits for them, and re-layouts  32.4 us (5%)
  between operations  14 us (2%)
  starting transfers between devices  12.4 us (2%)
    pallas_call x4, Pallas kernels, block_call(): pl.pallas_call(block_kernel, grid_spec=pltpu.PrefetchScalarGridSpec(num_s...  212 us
    pallas_call x4, Pallas kernels, attention_call(): pl.pallas_call(functools.partial(attention_kernel, head_dim=head_dim), gr...  193 us
    ppermute x15, waiting for transfers between devices, exchange(): lax.ppermute(piece, 'tp', [(i, i ^ k) for i in range(tp_size)])  118 us
    pallas_call x2, Pallas kernels, qkv_call(): pl.pallas_call(functools.partial(qkv_kernel, pieces=len(received), seq=se...  46.4 us
    pallas_call x1, Pallas kernels, next_qkv_call(): pl.pallas_call(next_qkv_kernel, grid=(tokens // BLOCK_TOKENS,), in_specs=...  37.2 us
  transfers between devices with their start and end apart: 23, of which 4 were waited for; matrix products, arithmetic and copies ran while one was open for 4% of the time, Pallas kernels for 57%

profile of v3, /device:TPU:0, one launch (start us, length us, event | category | flops | bytes accessed | tf_op | source)
XLA Modules:
  0.0 669.3 jit_solution(6440256727973286436)
XLA Ops:
  6.5 1.6 constant_dynamic-slice_fusion
  8.1 1.2 copy.23
  9.4 0.0 all-gather.18.cloned.1.call-start
  9.4 0.9 collective-permute-start.3
  10.3 2.5 collective-permute-start.4
  12.8 3.6 constant_dynamic-slice_fusion.7
  16.4 0.1 collective-permute-start
  16.5 1.7 collective-permute-start.1
  18.3 0.9 constant_dynamic-slice_fusion.5
  19.2 3.1 dynamic-slice_bitcast_fusion
  22.3 3.1 dynamic-slice_bitcast_fusion.1
  25.4 3.2 constant_dynamic-slice_fusion.1
  28.6 0.6 fusion.5
  29.3 0.6 fusion.3
  29.9 0.7 pad_add_fusion
  30.5 0.6 pad_add_fusion.2.rows_ref
  31.1 0.7 stack.51.place_ref
  31.8 1.2 copy.22
  33.0 0.5 collective-permute-start.5
  33.5 56.4 %collective-permute-done.5 = f32[2,1024]{1,0:T(2,128)S(1)} collective-permute-done((f32[2,1024]{1,0:T(2,128)S(1)}, f32[2,1024]{1,0:T(2,128)S(1)}, u32[]{:S(2)}, u32[]{:S(2)}) %collective-permute-start.5) | collective-permute-done | bytes 8224 | tf_op jit(solution)/shard_map/ppermute | solution.py:339
  89.9 0.6 copy.20
  90.6 0.6 copy.21
  91.3 0.7 all-gather.20.cloned.1.call-update
  92.0 0.5 all-gather.22.cloned.1.call-update
  92.6 1.9 collective-permute-start.7
  94.5 23.1 %ln_qkv.2 = (bf16[4,2048,768]{2,1,0:T(8,128)(2,1)}, bf16[4096,1024]{1,0:T(8,128)(2,1)}) custom-call(s32[5]{0:T(128)} %stack.51.place_ref, bf16[1,1,512,1024]{3,2,1,0:T(8,128)(2,1)} %collective-permute-done.refs_0_, bf16[1,1,512,1024]{3,2,1,0:T(8,128)(2,1)} %collective-permute-done.1.refs_1_, bf16[1,1,512,1024]{3,2,1,0:T(8,128)(2,1)} %collective-permute-done.2.refs_2_, ...), custom_call_target="tpu_custom_call" | custom-call | flops 12884901888 | bytes 23068672 | tf_op jit(solution)/shard_map/ln_qkv/pallas_call | solution.py:128
  117.7 48.0 %causal_attention.4.refs_3_ = bf16[4096,1024]{1,0:T(8,128)(2,1)} custom-call(bf16[4,2048,768]{2,1,0:T(8,128)(2,1)} %get-tuple-element.58.refs_0_.refs_1_.refs_2_, bf16[4,2048,768]{2,1,0:T(8,128)(2,1)} %get-tuple-element.58.refs_0_.refs_1_.refs_2_, bf16[4,2048,768]{2,1,0:T(8,128)(2,1)} %get-tuple-element.58.refs_0_.refs_1_.refs_2_), custom_call_target="tpu_custom_call" | custom-call | flops 28991029248 | bytes 16777216 | tf_op jit(solution)/shard_map/causal_attention/pallas_call | solution.py:214
  165.8 0.0 all-gather.26.cloned.1.call-start
  165.8 0.5 all-gather.26.cloned.1.call-update
  166.4 0.7 all-gather.28.cloned.1.call-update
  167.1 0.5 all-gather.30.cloned.1.call-start
  167.6 0.2 all-gather.30.cloned.1.call-update
  167.8 23.3 %ln_qkv.3 = (bf16[4,2048,768]{2,1,0:T(8,128)(2,1)}, bf16[4096,1024]{1,0:T(8,128)(2,1)}) custom-call(s32[5]{0:T(128)} %stack.51.place_ref, bf16[1,1,512,1024]{3,2,1,0:T(8,128)(2,1)} %copy-done.10, bf16[1,1,512,1024]{3,2,1,0:T(8,128)(2,1)} %collective-permute-done.7.refs_1_, ...), custom_call_target="tpu_custom_call", output_to_operand_aliasing={{1}: (8, {})} | custom-call | flops 12884901888 | bytes 23068672 | tf_op jit(solution)/shard_map/ln_qkv/pallas_call | solution.py:128
  191.1 48.2 %causal_attention.5.o_ref = bf16[4096,1024]{1,0:T(8,128)(2,1)} custom-call(bf16[4,2048,768]{2,1,0:T(8,128)(2,1)} %get-tuple-element.71.refs_0_.refs_1_.refs_2_, bf16[4,2048,768]{2,1,0:T(8,128)(2,1)} %get-tuple-element.71.refs_0_.refs_1_.refs_2_, bf16[4,2048,768]{2,1,0:T(8,128)(2,1)} %get-tuple-element.71.refs_0_.refs_1_.refs_2_, ...), custom_call_target="tpu_custom_call", output_to_operand_aliasing={{}: (3, {})} | custom-call | flops 28991029248 | bytes 16777216 | tf_op jit(solution)/shard_map/causal_attention/pallas_call | solution.py:214
  239.3 0.5 iota.3.rows_ref
  239.8 99.3 %ffn.4.r_ref = f32[4096,1024]{1,0:T(8,128)} custom-call(s32[8]{0:T(128)} %iota.3.rows_ref, bf16[4096,1024]{1,0:T(8,128)(2,1)} %get-tuple-element.70.r_ref, bf16[4096,1024]{1,0:T(8,128)(2,1)} %causal_attention.5.o_ref, f32[1,1024]{1,0:T(1,128)} %get-tuple-element.56.refs_4_.gain_ref, f32[1,1024]{1,0:T(1,128)} %get-tuple-element.57.refs_5_.bias_ref, ...), custom_call_target="tpu_custom_call" | custom-call | flops 77309411328 | bytes 33554432 | tf_op jit(solution)/shard_map/ffn/pallas_call | solution.py:288
  339.2 37.2 %next_qkv.1.refs_0_.refs_1_.refs_2_ = bf16[4,4096,768]{2,1,0:T(8,128)(2,1)} custom-call(f32[4096,1024]{1,0:T(8,128)} %ffn.4.r_ref, f32[1,1024]{1,0:T(1,128)} %get-tuple-element.75.gain_ref, f32[1,1024]{1,0:T(1,128)} %get-tuple-element.76.bias_ref, bf16[8,512,768]{2,1,0:T(8,128)(2,1)} %bitcast.79), custom_call_target="tpu_custom_call" | custom-call | flops 25769803776 | bytes 41943040 | tf_op jit(solution)/shard_map/next_qkv/pallas_call | solution.py:79
  376.4 48.2 %causal_attention.6.o_ref.refs_3_ = bf16[4096,1024]{1,0:T(8,128)(2,1)} custom-call(bf16[4,4096,768]{2,1,0:T(8,128)(2,1)} %next_qkv.1.refs_0_.refs_1_.refs_2_, bf16[4,4096,768]{2,1,0:T(8,128)(2,1)} %next_qkv.1.refs_0_.refs_1_.refs_2_, bf16[4,4096,768]{2,1,0:T(8,128)(2,1)} %next_qkv.1.refs_0_.refs_1_.refs_2_), custom_call_target="tpu_custom_call" | custom-call | flops 28991029248 | bytes 16777216 | tf_op jit(solution)/shard_map/causal_attention/pallas_call | solution.py:214
  424.6 29.9 %ffn.5 = bf16[1024,1024]{1,0:T(8,128)(2,1)} custom-call(s32[2]{0:T(128)} %get-tuple-element.78.rows_ref, f32[4096,1024]{1,0:T(8,128)} %ffn.4.r_ref, bf16[4096,1024]{1,0:T(8,128)(2,1)} %causal_attention.6.o_ref.refs_3_, f32[1,1024]{1,0:T(1,128)} %get-tuple-element.75.gain_ref, f32[1,1024]{1,0:T(1,128)} %get-tuple-element.76.bias_ref, ...), custom_call_target="tpu_custom_call" | custom-call | flops 19327352832 | bytes 8388608 | tf_op jit(solution)/shard_map/ffn/pallas_call | solution.py:288
  454.5 48.4 %causal_attention.7.o_ref = bf16[4096,1024]{1,0:T(8,128)(2,1)} custom-call(bf16[4,4096,768]{2,1,0:T(8,128)(2,1)} %next_qkv.1.refs_0_.refs_1_.refs_2_, bf16[4,4096,768]{2,1,0:T(8,128)(2,1)} %next_qkv.1.refs_0_.refs_1_.refs_2_, bf16[4,4096,768]{2,1,0:T(8,128)(2,1)} %next_qkv.1.refs_0_.refs_1_.refs_2_, ...), custom_call_target="tpu_custom_call", output_to_operand_aliasing={{}: (3, {})} | custom-call | flops 28991029248 | bytes 16777216 | tf_op jit(solution)/shard_map/causal_attention/pallas_call | solution.py:214
  502.9 30.2 %ffn.6 = bf16[1024,1024]{1,0:T(8,128)(2,1)} custom-call(s32[2]{0:T(128)} %get-tuple-element.87.rows_ref, f32[4096,1024]{1,0:T(8,128)} %ffn.4.r_ref, bf16[4096,1024]{1,0:T(8,128)(2,1)} %causal_attention.7.o_ref, f32[1,1024]{1,0:T(1,128)} %get-tuple-element.75.gain_ref, f32[1,1024]{1,0:T(1,128)} %get-tuple-element.76.bias_ref, ...), custom_call_target="tpu_custom_call" | custom-call | flops 19327352832 | bytes 8388608 | tf_op jit(solution)/shard_map/ffn/pallas_call | solution.py:288
  533.1 1.2 slice_bitcast_fusion.6
  534.3 0.8 collective-permute-start.9
  535.2 52.8 %ffn.7 = bf16[2048,1024]{1,0:T(8,128)(2,1)} custom-call(s32[4]{0:T(128)} %pad_add_fusion.2.rows_ref, f32[4096,1024]{1,0:T(8,128)} %ffn.4.r_ref, bf16[4096,1024]{1,0:T(8,128)(2,1)} %causal_attention.7.o_ref, f32[1,1024]{1,0:T(1,128)} %get-tuple-element.75.gain_ref, f32[1,1024]{1,0:T(1,128)} %get-tuple-element.76.bias_ref, ...), custom_call_target="tpu_custom_call" | custom-call | flops 38654705664 | bytes 16777216 | tf_op jit(solution)/shard_map/ffn/pallas_call | solution.py:288
  587.9 1.1 collective-permute-start.10
  589.1 1.5 slice_bitcast_fusion.4
  590.6 0.5 collective-permute-start.11
  591.1 1.1 collective-permute-start.12
  592.1 2.7 slice_bitcast_fusion.1
  594.8 0.4 collective-permute-start.13
  595.2 0.2 collective-permute-start.14
  595.4 1.1 broadcast_in_dim.18
  596.4 0.1 constant_dynamic-update-slice_fusion.5
  596.5 17.4 %collective-permute-done.10 = bf16[1,1,512,1024]{3,2,1,0:T(8,128)(2,1)S(1)} collective-permute-done((bf16[1,1,512,1024]{3,2,1,0:T(8,128)(2,1)S(1)}, bf16[1,1,512,1024]{3,2,1,0:T(8,128)(2,1)S(1)}, u32[]{:S(2)}, u32[]{:S(2)}) %collective-permute-start.10) | collective-permute-done | bytes 1048608 | tf_op jit(solution)/shard_map/ppermute | solution.py:339
  614.0 0.1 constant_dynamic-update-slice_fusion.4
  614.1 21.1 %collective-permute-done.11 = bf16[1,1,512,1024]{3,2,1,0:T(8,128)(2,1)S(1)} collective-permute-done((bf16[1,1,512,1024]{3,2,1,0:T(8,128)(2,1)}, bf16[1,1,512,1024]{3,2,1,0:T(8,128)(2,1)S(1)}, u32[]{:S(2)}, u32[]{:S(2)}) %collective-permute-start.11) | collective-permute-done | bytes 1048608 | tf_op jit(solution)/shard_map/ppermute | solution.py:339
  635.2 0.1 constant_dynamic-update-slice_fusion.3
  635.3 22.9 %collective-permute-done.12 = bf16[1,1,512,1024]{3,2,1,0:T(8,128)(2,1)S(1)} collective-permute-done((bf16[1,1,512,1024]{3,2,1,0:T(8,128)(2,1)}, bf16[1,1,512,1024]{3,2,1,0:T(8,128)(2,1)S(1)}, u32[]{:S(2)}, u32[]{:S(2)}) %collective-permute-start.12) | collective-permute-done | bytes 1048608 | tf_op jit(solution)/shard_map/ppermute | solution.py:339
  658.2 0.1 constant_dynamic-update-slice_fusion.2
  658.3 0.1 constant_dynamic-update-slice_fusion.1
  658.5 0.1 fusion.1
  658.6 0.1 constant_dynamic-update-slice_fusion
  658.7 0.1 fusion
  658.8 3.4 copy-done
  (59 shorter events, 0.5 us)
Async XLA Ops:
  6.5 11.8 %copy-start.5 = (f32[2,1024]{1,0:T(2,128)S(1)}, f32[2,1024]{1,0:T(2,128)}, u32[]{:S(2)}) copy-start(f32[2,1024]{1,0:T(2,128)} %param.15) | copy-start | bytes 24580
  6.5 11.8 %copy-start.6 = (f32[2,1024]{1,0:T(2,128)S(1)}, f32[2,1024]{1,0:T(2,128)}, u32[]{:S(2)}) copy-start(f32[2,1024]{1,0:T(2,128)} %param.19) | copy-start | bytes 24580
  6.5 11.8 %copy-start.4 = (bf16[2,4,64,1024]{3,2,1,0:T(8,128)(2,1)S(1)}, bf16[2,4,64,1024]{3,2,1,0:T(8,128)(2,1)}, u32[]{:S(2)}) copy-start(bf16[2,4,64,1024]{3,2,1,0:T(8,128)(2,1)} %param.14) | copy-start | bytes 3145732
  6.5 88.0 %all-gather.16.cloned.1.call-start = ((), (), s32[]{:S(2)}) async-start(), calls=%async_computation | async-start | bytes 7077888 | tf_op jit(solution)/shard_map/all_gather | solution.py:322
  9.4 229.9 %all-gather.18.cloned.1.call-start = ((), (), s32[]{:S(2)}) async-start(), calls=%async_computation.1 | async-start | bytes 2359296 | tf_op jit(solution)/shard_map/all_gather | solution.py:322
  9.4 23.6 %collective-permute-start.3 = (f32[2,1024]{1,0:T(2,128)}, f32[2,1024]{1,0:T(2,128)S(1)}, u32[]{:S(2)}, u32[]{:S(2)}) collective-permute-start(f32[2,1024]{1,0:T(2,128)} %param.17), channel_id=1, source_target_pairs={{0,1},{1,0},{2,3},{3,2},{4,5},{5,4},{6,7},{7,6}} | collective-permute-start | bytes 24584 | tf_op jit(solution)/shard_map/ppermute | solution.py:339
  10.3 23.2 %collective-permute-start.4 = (f32[2,1024]{1,0:T(2,128)}, f32[2,1024]{1,0:T(2,128)S(1)}, u32[]{:S(2)}, u32[]{:S(2)}) collective-permute-start(f32[2,1024]{1,0:T(2,128)} %param.17), channel_id=1, source_target_pairs={{0,2},{1,3},{2,0},{3,1},{4,6},{5,7},{6,4},{7,5}} | collective-permute-start | bytes 24584 | tf_op jit(solution)/shard_map/ppermute | solution.py:339
  16.4 12.2 %copy-start.7 = (f32[2,1024]{1,0:T(2,128)S(1)}, f32[2,1024]{1,0:T(2,128)}, u32[]{:S(2)}) copy-start(f32[2,1024]{1,0:T(2,128)} %param.11) | copy-start | bytes 24580
  16.4 12.8 %copy-start.8 = (f32[2,1024]{1,0:T(2,128)S(1)}, f32[2,1024]{1,0:T(2,128)}, u32[]{:S(2)}) copy-start(f32[2,1024]{1,0:T(2,128)} %param.17) | copy-start | bytes 24580
  16.4 12.8 %copy-start.9 = (f32[2,1024]{1,0:T(2,128)S(1)}, f32[2,1024]{1,0:T(2,128)}, u32[]{:S(2)}) copy-start(f32[2,1024]{1,0:T(2,128)} %param.12) | copy-start | bytes 24580
  16.4 74.7 %collective-permute-start = (bf16[1,1,512,1024]{3,2,1,0:T(8,128)(2,1)}, bf16[1,1,512,1024]{3,2,1,0:T(8,128)(2,1)}, u32[]{:S(2)}, u32[]{:S(2)}) collective-permute-start(bf16[1,1,512,1024]{3,2,1,0:T(8,128)(2,1)} %get-tuple-element.96), channel_id=1, source_target_pairs={{0,3},{1,2},{2,1},{3,0},{4,7},{5,6},{6,5},{7,4}} | collective-permute-start | bytes 3145736 | tf_op jit(solution)/shard_map/ppermute | solution.py:339
  16.5 74.6 %collective-permute-start.1 = (bf16[1,1,512,1024]{3,2,1,0:T(8,128)(2,1)}, bf16[1,1,512,1024]{3,2,1,0:T(8,128)(2,1)}, u32[]{:S(2)}, u32[]{:S(2)}) collective-permute-start(bf16[1,1,512,1024]{3,2,1,0:T(8,128)(2,1)} %get-tuple-element.95), channel_id=1, source_target_pairs={{0,2},{1,3},{2,0},{3,1},{4,6},{5,7},{6,4},{7,5}} | collective-permute-start | bytes 3145736 | tf_op jit(solution)/shard_map/ppermute | solution.py:339
  18.3 72.9 %collective-permute-start.2 = (bf16[1,1,512,1024]{3,2,1,0:T(8,128)(2,1)}, bf16[1,1,512,1024]{3,2,1,0:T(8,128)(2,1)}, u32[]{:S(2)}, u32[]{:S(2)}) collective-permute-start(bf16[1,1,512,1024]{3,2,1,0:T(8,128)(2,1)} %get-tuple-element.94), channel_id=1, source_target_pairs={{0,1},{1,0},{2,3},{3,2},{4,5},{5,4},{6,7},{7,6}} | collective-permute-start | bytes 3145736 | tf_op jit(solution)/shard_map/ppermute | solution.py:339
  33.0 56.9 %collective-permute-start.5 = (f32[2,1024]{1,0:T(2,128)S(1)}, f32[2,1024]{1,0:T(2,128)S(1)}, u32[]{:S(2)}, u32[]{:S(2)}) collective-permute-start(f32[2,1024]{1,0:T(2,128)S(1)} %copy-done.8), channel_id=1, source_target_pairs={{0,3},{1,2},{2,1},{3,0},{4,7},{5,6},{6,5},{7,4}} | collective-permute-start | bytes 24584 | tf_op jit(solution)/shard_map/ppermute | solution.py:339
  91.2 148.1 %all-gather.20.cloned.1.call-start = ((), (), s32[]{:S(2)}) async-start(), calls=%async_computation.2 | async-start | bytes 9437184 | tf_op jit(solution)/shard_map/all_gather | solution.py:322
  91.9 147.4 %all-gather.22.cloned.1.call-start = ((), (), s32[]{:S(2)}) async-start(), calls=%async_computation.3 | async-start | bytes 9437184 | tf_op jit(solution)/shard_map/all_gather | solution.py:322
  92.5 246.7 %all-gather.24.cloned.1.call-start = ((), (), s32[]{:S(2)}) async-start(), calls=%async_computation.4 | async-start | bytes 7077888 | tf_op jit(solution)/shard_map/all_gather | solution.py:322
  92.6 73.1 %collective-permute-start.6 = (bf16[1,1,512,1024]{3,2,1,0:T(8,128)(2,1)}, bf16[1,1,512,1024]{3,2,1,0:T(8,128)(2,1)S(1)}, u32[]{:S(2)}, u32[]{:S(2)}) collective-permute-start(bf16[1,1,512,1024]{3,2,1,0:T(8,128)(2,1)} %get-tuple-element.50), channel_id=1, source_target_pairs={{0,3},{1,2},{2,1},{3,0},{4,7},{5,6},{6,5},{7,4}} | collective-permute-start | bytes 3145736 | tf_op jit(solution)/shard_map/ppermute | solution.py:339
  92.6 73.1 %collective-permute-start.7 = (bf16[1,1,512,1024]{3,2,1,0:T(8,128)(2,1)S(1)}, bf16[1,1,512,1024]{3,2,1,0:T(8,128)(2,1)}, u32[]{:S(2)}, u32[]{:S(2)}) collective-permute-start(bf16[1,1,512,1024]{3,2,1,0:T(8,128)(2,1)S(1)} %get-tuple-element.51), channel_id=1, source_target_pairs={{0,2},{1,3},{2,0},{3,1},{4,6},{5,7},{6,4},{7,5}} | collective-permute-start | bytes 3145736 | tf_op jit(solution)/shard_map/ppermute | solution.py:339
  94.5 71.2 %collective-permute-start.8 = (bf16[1,1,512,1024]{3,2,1,0:T(8,128)(2,1)S(1)}, bf16[1,1,512,1024]{3,2,1,0:T(8,128)(2,1)}, u32[]{:S(2)}, u32[]{:S(2)}) collective-permute-start(bf16[1,1,512,1024]{3,2,1,0:T(8,128)(2,1)S(1)} %get-tuple-element.52), channel_id=1, source_target_pairs={{0,1},{1,0},{2,3},{3,2},{4,5},{5,4},{6,7},{7,6}} | collective-permute-start | bytes 3145736 | tf_op jit(solution)/shard_map/ppermute | solution.py:339
  165.7 2.1 copy-start.10
  165.8 258.9 %all-gather.26.cloned.1.call-start = ((), (), s32[]{:S(2)}) async-start(), calls=%async_computation.5 | async-start | bytes 2359296 | tf_op jit(solution)/shard_map/all_gather | solution.py:322
  166.3 258.3 %all-gather.28.cloned.1.call-start = ((), (), s32[]{:S(2)}) async-start(), calls=%async_computation.6 | async-start | bytes 9437184 | tf_op jit(solution)/shard_map/all_gather | solution.py:322
  167.1 257.5 %all-gather.30.cloned.1.call-start = ((), (), s32[]{:S(2)}) async-start(), calls=%async_computation.7 | async-start | bytes 9437184 | tf_op jit(solution)/shard_map/all_gather | solution.py:322
  502.9 30.2 %copy-start.3 = (bf16[1024,1024]{1,0:T(8,128)(2,1)S(1)}, bf16[1024,1024]{1,0:T(8,128)(2,1)}, u32[]{:S(2)}) copy-start(bf16[1024,1024]{1,0:T(8,128)(2,1)} %ffn.5) | copy-start | bytes 6291460
  534.3 54.8 %copy-start.2 = (bf16[1024,1024]{1,0:T(8,128)(2,1)S(1)}, bf16[1024,1024]{1,0:T(8,128)(2,1)}, u32[]{:S(2)}) copy-start(bf16[1024,1024]{1,0:T(8,128)(2,1)} %ffn.6) | copy-start | bytes 6291460
  534.3 60.9 %collective-permute-start.9 = (bf16[1,1,512,1024]{3,2,1,0:T(8,128)(2,1)}, bf16[1,1,512,1024]{3,2,1,0:T(8,128)(2,1)S(1)}, u32[]{:S(2)}, u32[]{:S(2)}) collective-permute-start(bf16[1,1,512,1024]{3,2,1,0:T(8,128)(2,1)} %get-tuple-element.108), channel_id=1, source_target_pairs={{0,3},{1,2},{2,1},{3,0},{4,7},{5,6},{6,5},{7,4}} | collective-permute-start | bytes 3145736 | tf_op jit(solution)/shard_map/ppermute | solution.py:339
  587.9 26.1 %collective-permute-start.10 = (bf16[1,1,512,1024]{3,2,1,0:T(8,128)(2,1)S(1)}, bf16[1,1,512,1024]{3,2,1,0:T(8,128)(2,1)S(1)}, u32[]{:S(2)}, u32[]{:S(2)}) collective-permute-start(bf16[1,1,512,1024]{3,2,1,0:T(8,128)(2,1)S(1)} %get-tuple-element.107), channel_id=1, source_target_pairs={{0,2},{1,3},{2,0},{3,1},{4,6},{5,7},{6,4},{7,5}} | collective-permute-start | bytes 3145736 | tf_op jit(solution)/shard_map/ppermute | solution.py:339
  590.6 44.6 %collective-permute-start.11 = (bf16[1,1,512,1024]{3,2,1,0:T(8,128)(2,1)}, bf16[1,1,512,1024]{3,2,1,0:T(8,128)(2,1)S(1)}, u32[]{:S(2)}, u32[]{:S(2)}) collective-permute-start(bf16[1,1,512,1024]{3,2,1,0:T(8,128)(2,1)} %get-tuple-element.106), channel_id=1, source_target_pairs={{0,3},{1,2},{2,1},{3,0},{4,7},{5,6},{6,5},{7,4}} | collective-permute-start | bytes 3145736 | tf_op jit(solution)/shard_map/ppermute | solution.py:339
  591.1 67.1 %collective-permute-start.12 = (bf16[1,1,512,1024]{3,2,1,0:T(8,128)(2,1)}, bf16[1,1,512,1024]{3,2,1,0:T(8,128)(2,1)S(1)}, u32[]{:S(2)}, u32[]{:S(2)}) collective-permute-start(bf16[1,1,512,1024]{3,2,1,0:T(8,128)(2,1)} %get-tuple-element.105), channel_id=1, source_target_pairs={{0,2},{1,3},{2,0},{3,1},{4,6},{5,7},{6,4},{7,5}} | collective-permute-start | bytes 3145736 | tf_op jit(solution)/shard_map/ppermute | solution.py:339
  594.8 63.5 %collective-permute-start.13 = (bf16[1,1,512,1024]{3,2,1,0:T(8,128)(2,1)}, bf16[1,1,512,1024]{3,2,1,0:T(8,128)(2,1)S(1)}, u32[]{:S(2)}, u32[]{:S(2)}) collective-permute-start(bf16[1,1,512,1024]{3,2,1,0:T(8,128)(2,1)} %get-tuple-element.98), channel_id=1, source_target_pairs={{0,1},{1,0},{2,3},{3,2},{4,5},{5,4},{6,7},{7,6}} | collective-permute-start | bytes 3145736 | tf_op jit(solution)/shard_map/ppermute | solution.py:339
  595.2 63.3 %copy-start.1 = (bf16[2048,1024]{1,0:T(8,128)(2,1)S(1)}, bf16[2048,1024]{1,0:T(8,128)(2,1)}, u32[]{:S(2)}) copy-start(bf16[2048,1024]{1,0:T(8,128)(2,1)} %ffn.7) | copy-start | bytes 12582916
  595.2 63.4 %collective-permute-start.14 = (bf16[1,1,512,1024]{3,2,1,0:T(8,128)(2,1)S(1)}, bf16[1,1,512,1024]{3,2,1,0:T(8,128)(2,1)S(1)}, u32[]{:S(2)}, u32[]{:S(2)}) collective-permute-start(bf16[1,1,512,1024]{3,2,1,0:T(8,128)(2,1)S(1)} %get-tuple-element.97), channel_id=1, source_target_pairs={{0,1},{1,0},{2,3},{3,2},{4,5},{5,4},{6,7},{7,6}} | collective-permute-start | bytes 3145736 | tf_op jit(solution)/shard_map/ppermute | solution.py:339
  658.8 3.4 copy-start
Sparse Core Ops, SparseCore 0:
  9.5 67.4 all-gather.15
  91.3 30.7 all-gather.17
  123.9 60.4 all-gather.19
  186.2 48.7 all-gather.21
  236.6 39.8 all-gather.23
  278.2 22.2 all-gather.25
  302.2 48.6 all-gather.27
  352.8 48.6 all-gather.29
